TPU v7x, 16 devices: a 4x2x1 block of a 4x4x8 slice. The times are simulated.
16 devices in a mesh: dp: 2 (over y, z), tp: 8 (over x, core).
Axes of the slice: x: 4, y: 2, z: 1, core: 2. Of those that a mesh axis runs over, the one named last changes fastest.
The devices are a block of a 4x4x8 slice.
Arguments:
- hidden: bfloat16 [16, 584, 1024], P('dp'), parts along dimension 0
- inter_feats: bfloat16 [16, 584, 5, 1024], P('dp'), parts along dimension 0
- proj_grad: bfloat16 [16, 577, 4096], P('dp'), parts along dimension 0
- w_query: bfloat16 [1024, 16, 64], P(None, 'tp')
- w_key: bfloat16 [1024, 16, 64], P(None, 'tp')
- w_value: bfloat16 [1024, 16, 64], P(None, 'tp')
- w_out: bfloat16 [16, 64, 1024], P('tp')
- ln_params: float32 [4, 1024], replicated
- gate_params: float32 [2], replicated
- w_fc1: bfloat16 [1024, 4096], P(None, 'tp')
- b_fc1: float32 [4096], P('tp')
- w_fc2: bfloat16 [4096, 1024], P('tp')
- b_fc2: float32 [1024], replicated
- w_proj: bfloat16 [6144, 4096], P('tp')
- b_proj: float32 [4096], replicated
Outputs:
- output 1: bfloat16 [16, 577, 4096], P(('dp', 'tp')), parts along dimension 0
- output 2: bfloat16 [16, 584, 1024], P('dp'), parts along dimension 0
- output 3: bfloat16 [16, 584, 5, 1024], P('dp'), parts along dimension 0
- output 4: float32 [2048, 16, 64], P('dp', 'tp'), parts along dimension 0
- output 5: float32 [2048, 16, 64], P('dp', 'tp'), parts along dimension 0
- output 6: float32 [2048, 16, 64], P('dp', 'tp'), parts along dimension 0
- output 7: float32 [32, 64, 1024], P(('dp', 'tp')), parts along dimension 0
- output 8: float32 [8, 1024], P('dp'), parts along dimension 0
- output 9: float32 [4], P('dp'), parts along dimension 0
- output 10: float32 [2048, 4096], P('dp', 'tp'), parts along dimension 0
- output 11: float32 [8192], P(('dp', 'tp')), parts along dimension 0
- output 12: float32 [8192, 1024], P(('dp', 'tp')), parts along dimension 0
- output 13: float32 [2048], P('dp'), parts along dimension 0
- output 14: float32 [12288, 4096], P(('dp', 'tp')), parts along dimension 0
- output 15: float32 [8192], P('dp'), parts along dimension 0
There are 2 independent parts. A program takes and returns all parts, laid end to end along the dimension named above; an argument that names none is the same for every part.
All inputs are finite; a program needn't handle non-finite values.
Results may differ from a plain program's by a relative error of at most 0.0185521.
Values are sent between devices in bfloat16 or wider.
A program may use at most 768 MiB of HBM per device.

v0:
```python
import functools
import jax
import jax.numpy as jnp
from jax import lax
from jax.sharding import PartitionSpec as P

LN_EPS = 1e-5


def layer_norm(values, ln_gain, ln_bias):
    row_mean = jnp.mean(values, axis=-1, keepdims=True)
    centred = values - row_mean
    row_var = jnp.mean(centred * centred, axis=-1, keepdims=True)
    return (centred * lax.rsqrt(row_var + LN_EPS) * ln_gain + ln_bias).astype(jnp.bfloat16)


def gelu_bf16(pre_act):
    return jax.nn.gelu(pre_act, approximate=False).astype(jnp.bfloat16)


def matmul(eq_form, lhs_in, rhs_in):
    return jnp.einsum(eq_form, lhs_in, rhs_in, preferred_element_type=jnp.float32)


def attend(real_rows, q_act, k_act, v_act):
    tokens = q_act.shape[1]
    score_scale = q_act.shape[3] ** -0.5
    scores = matmul('bqhe,bkhe->bhqk', q_act, k_act) * score_scale
    key_ok = (jnp.arange(tokens) < real_rows)[None, None, None, :]
    attn_probs = jax.nn.softmax(jnp.where(key_ok, scores, -1e30), axis=-1).astype(jnp.bfloat16)
    return matmul('bhqk,bkhe->bqhe', attn_probs, v_act).astype(jnp.bfloat16)


def group_sum(part_sum):
    return lax.psum(part_sum.astype(jnp.bfloat16), 'tp').astype(jnp.float32)


def local_step(hidden, inter_feats, proj_grad, w_query, w_key, w_value, w_out, ln_params, gate_params, w_fc1, b_fc1, w_fc2, b_fc2, w_proj, b_proj):
    tile_count, tokens, width = hidden.shape
    real_rows = proj_grad.shape[1]
    feat_local = w_proj.shape[0]
    x_wide = hidden.astype(jnp.float32)
    normed, norm1_pull = jax.vjp(layer_norm, x_wide, ln_params[0], ln_params[1])
    q_act = matmul('btd,dhe->bthe', normed, w_query).astype(jnp.bfloat16)
    k_act = matmul('btd,dhe->bthe', normed, w_key).astype(jnp.bfloat16)
    v_act = matmul('btd,dhe->bthe', normed, w_value).astype(jnp.bfloat16)
    context, attend_pull = jax.vjp(functools.partial(attend, real_rows), q_act, k_act, v_act)
    attn_out = group_sum(matmul('bthe,hed->btd', context, w_out))
    gate_attn = jnp.tanh(gate_params[0])
    gate_mlp = jnp.tanh(gate_params[1])
    x_one = (x_wide + gate_attn * attn_out).astype(jnp.bfloat16)
    x_one_wide = x_one.astype(jnp.float32)
    normed_two, norm2_pull = jax.vjp(layer_norm, x_one_wide, ln_params[2], ln_params[3])
    pre_act = matmul('btd,df->btf', normed_two, w_fc1) + b_fc1
    mlp_act, gelu_pull = jax.vjp(gelu_bf16, pre_act)
    mlp_out = group_sum(matmul('btf,fd->btd', mlp_act, w_fc2)) + b_fc2
    x_two = (x_one_wide + gate_mlp * mlp_out).astype(jnp.bfloat16)
    features = jnp.concatenate([x_two[:, :real_rows], inter_feats[:, :real_rows].reshape(tile_count, real_rows, -1)], axis=-1)
    feats_local = lax.dynamic_slice_in_dim(features, lax.axis_index('tp') * feat_local, feat_local, axis=2)
    proj_part = matmul('btc,cp->btp', feats_local, w_proj).astype(jnp.bfloat16)
    proj_sum = lax.psum_scatter(proj_part, 'tp', scatter_dimension=0, tiled=True)
    proj_out = (proj_sum.astype(jnp.float32) + b_proj).astype(jnp.bfloat16)

    grad_b_proj = jnp.sum(proj_grad, axis=(0, 1), dtype=jnp.float32)
    grad_w_proj = matmul('btc,btp->cp', feats_local, proj_grad)
    grad_feats_local = matmul('btp,cp->btc', proj_grad, w_proj).astype(jnp.bfloat16)
    grad_feats = lax.all_gather(grad_feats_local, 'tp', axis=2, tiled=True)
    pad_rows = ((0, 0), (0, tokens - real_rows), (0, 0))
    grad_x_two = jnp.pad(grad_feats[:, :, :width], pad_rows).astype(jnp.float32)
    grad_inter = jnp.pad(grad_feats[:, :, width:], pad_rows).reshape(inter_feats.shape)
    grad_mlp = gate_mlp * grad_x_two
    grad_gate_mlp = jnp.sum(grad_x_two * mlp_out) * (1.0 - gate_mlp * gate_mlp)
    grad_b_fc2 = jnp.sum(grad_mlp, axis=(0, 1))
    grad_mlp_low = grad_mlp.astype(jnp.bfloat16)
    grad_w_fc2 = matmul('btf,btd->fd', mlp_act, grad_mlp_low)
    grad_act = matmul('btd,fd->btf', grad_mlp_low, w_fc2).astype(jnp.bfloat16)
    grad_pre = gelu_pull(grad_act)[0]
    grad_b_fc1 = jnp.sum(grad_pre, axis=(0, 1))
    grad_pre_low = grad_pre.astype(jnp.bfloat16)
    grad_w_fc1 = matmul('btd,btf->df', normed_two, grad_pre_low)
    grad_normed_two = group_sum(matmul('btf,df->btd', grad_pre_low, w_fc1)).astype(jnp.bfloat16)
    grad_x_ln_two, grad_gain_two, grad_bias_two = norm2_pull(grad_normed_two)
    grad_x_one = (grad_x_two + grad_x_ln_two).astype(jnp.bfloat16).astype(jnp.float32)
    grad_attn = gate_attn * grad_x_one
    grad_gate_attn = jnp.sum(grad_x_one * attn_out) * (1.0 - gate_attn * gate_attn)
    grad_attn_low = grad_attn.astype(jnp.bfloat16)
    grad_w_out = matmul('bthe,btd->hed', context, grad_attn_low)
    grad_context = matmul('btd,hed->bthe', grad_attn_low, w_out).astype(jnp.bfloat16)
    grad_q, grad_k, grad_v = attend_pull(grad_context)
    grad_w_query = matmul('btd,bthe->dhe', normed, grad_q)
    grad_w_key = matmul('btd,bthe->dhe', normed, grad_k)
    grad_w_value = matmul('btd,bthe->dhe', normed, grad_v)
    grad_normed_sum = matmul('bthe,dhe->btd', grad_q, w_query) + matmul('bthe,dhe->btd', grad_k, w_key) + matmul('bthe,dhe->btd', grad_v, w_value)
    grad_normed = group_sum(grad_normed_sum).astype(jnp.bfloat16)
    grad_x_ln, grad_gain, grad_bias = norm1_pull(grad_normed)
    grad_hidden = (grad_x_one + grad_x_ln).astype(jnp.bfloat16)
    grad_ln = jnp.stack([grad_gain, grad_bias, grad_gain_two, grad_bias_two])
    grad_gates = jnp.stack([grad_gate_attn, grad_gate_mlp])
    return (proj_out, grad_hidden, grad_inter, grad_w_query, grad_w_key, grad_w_value, grad_w_out, grad_ln, grad_gates, grad_w_fc1, grad_b_fc1, grad_w_fc2, grad_b_fc2, grad_w_proj, grad_b_proj)


def solution(mesh):
    tiles_spec = P('dp', None, None)
    inter_spec = P('dp', None, None, None)
    head_cols = P(None, 'tp', None)
    in_specs = (tiles_spec, inter_spec, tiles_spec, head_cols, head_cols, head_cols, P('tp', None, None), P(None, None), P(None), P(None, 'tp'), P('tp'), P('tp', None), P(None), P('tp', None), P(None))
    grad_heads = P('dp', 'tp', None)
    out_specs = (P(('dp', 'tp'), None, None), tiles_spec, inter_spec, grad_heads, grad_heads, grad_heads, P(('dp', 'tp'), None, None), P('dp', None), P('dp'), P('dp', 'tp'), P(('dp', 'tp')), P(('dp', 'tp'), None), P('dp'), P(('dp', 'tp'), None), P('dp'))
    return jax.shard_map(local_step, mesh=mesh, in_specs=in_specs, out_specs=out_specs, check_vma=False)
```

profile of v0, /device:TPU:112, one launch (start us, length us, event | category | flops | bytes accessed | tf_op | source)
XLA Modules:
  0.0 1368.8 jit_solution(16292902807476162530)
XLA Ops:
  8.3 5.3 convert_reduce_fusion.3
  33.8 15.3 %fusion.127 = (f32[8,2,584]{2,1,0:T(2,128)S(1)}, f32[8,2,584,584]{2,3,1,0:T(8,128)}) fusion(pred[584]{0:T(1024)(128)(4,1)S(1)} %iota_compare_fusion, bf16[8,584,2,64]{1,3,2,0:T(8,128)(2,1)} %convolution_convert_fusion.9, bf16[8,584,2,64]{1,3,2,0:T(8,128)(2,1)} %convolution_convert_fusion.8), kind=kOutput, calls=%fused_computation.182 | convolution fusion | flops 720310848 | bytes 24257608 | tf_op jit(solution)/shard_map/jvp()/sub | solution.py:30
  49.1 9.2 divide_convert_fusion
  66.3 5.2 bitcast_convert_fusion
  71.6 36.8 %fusion.66 = bf16[8,577,768]{2,0,1:T(8,128)(2,1)} fusion(bf16[8,577,4096]{2,0,1:T(8,128)(2,1)} %param.17, bf16[768,4096]{1,0:T(8,128)(2,1)} %param.28), kind=kOutput, calls=%fused_computation.117 | convolution fusion | flops 29041360896 | bytes 51195904 | tf_op jit(solution)/shard_map/btp,cp->btc/dot_general | solution.py:22
  108.4 7.4 copy.79
  117.9 63.7 %all-reduce.7.cloned.1.call-done = bf16[8,584,1024]{2,1,0:T(8,128)(2,1)} async-done(((bf16[8,584,1024]{2,1,0:T(8,128)(2,1)}), bf16[8,584,1024]{2,1,0:T(8,128)(2,1)}) %all-reduce.7.cloned.1.call-update) | async-done | bytes 9568272 | tf_op jit(solution)/shard_map/psum | solution.py:35
  181.5 8.7 convert_reduce_fusion.4
  193.0 10.6 fusion.80
  207.3 23.0 %multiply_convert_fusion = (bf16[8,584,512]{2,1,0:T(8,128)(2,1)}, f32[8,584,512]{2,1,0:T(8,128)}) fusion(f32[8,584,512]{2,1,0:T(8,128)S(1)} %get-tuple-element.72, f32[512]{0:T(512)S(1)} %copy-done.50, u8[584,512]{1,0:T(8,128)(4,1)S(1)} %get-tuple-element.50, u8[584,512]{1,0:T(8,128)(4,1)S(1)} %get-tuple-element.49), kind=kLoop, calls=%fused_computation.95 | loop fusion | flops 169836544 | bytes 24520704 | tf_op jit(solution)/shard_map/jvp()/convert_element_type | solution.py:18
  230.3 205.8 %all-gather.2.cloned.1.call-done = bf16[8,577,6144]{2,1,0:T(8,128)(2,1)} async-done(((bf16[8,577,768]{2,1,0:T(8,128)(2,1)}), bf16[8,577,6144]{2,1,0:T(8,128)(2,1)}) %all-gather.2.cloned.1.call-update) | async-done | bytes 56721424 | tf_op jit(solution)/shard_map/all_gather | solution.py:67
  436.1 8.6 slice.42
  444.7 15.3 %fusion.128 = (f32[512]{0:T(512)}, bf16[8,584,512]{2,1,0:T(8,128)(2,1)S(1)}) fusion(f32[8,584,512]{2,1,0:T(8,128)} %get-tuple-element.60, bf16[512,1024]{1,0:T(8,128)(2,1)S(1)} %copy-done.54, f32[]{:T(128)} %bitcast.13, bf16[8,577,1024]{2,1,0:T(8,128)(2,1)} %slice.42, f32[8,584,512]{2,1,0:T(8,128)} %copy-done.14, f32[512]{0:T(512)S(1)} %copy-done.50), kind=kOutput, calls=%fused_computation.183 | convolution fusion | flops 4956356096 | bytes 34426884 | tf_op jit(solution)/shard_map/btd,fd->btf/dot_general | solution.py:22
  462.2 8.1 convolution_convert_fusion.2
  471.1 10.0 convolution_convert_fusion.3
  481.1 96.3 %all-reduce.9.cloned.1.call-done = bf16[8,584,1024]{2,1,0:T(8,128)(2,1)} async-done(((bf16[8,584,1024]{2,1,0:T(8,128)(2,1)}), bf16[8,584,1024]{2,1,0:T(8,128)(2,1)}) %all-reduce.9.cloned.1.call-update) | async-done | bytes 9568272 | tf_op jit(solution)/shard_map/psum | solution.py:35
  577.4 10.5 fusion.21
  588.0 13.1 fusion.27
  601.1 16.5 %fusion.30 = (f32[]{:T(128)}, bf16[8,584,1024]{2,1,0:T(8,128)(2,1)S(1)}) fusion(bf16[8,584,1024]{2,1,0:T(8,128)(2,1)} %all-reduce.7.cloned.1.call-done, f32[8,584]{1,0:T(8,128)S(1)} %negate_multiply_fusion.2, f32[8,584]{1,0:T(8,128)S(1)} %multiply_multiply_fusion.6, f32[8,584]{1,0:T(8,128)S(1)} %broadcast_multiply_fusion, ...), kind=kLoop, calls=%fused_computation.57 | loop fusion | flops 76546048 | bytes 47805444 | tf_op jit(solution)/shard_map/reduce_sum | solution.py:85
  625.8 9.2 fusion.91
  634.9 14.0 %fusion.12 = (f32[8,2,584]{2,1,0:T(2,128)S(1)}, bf16[8,2,584,584]{2,3,1,0:T(8,128)(2,1)}) fusion(f32[8,2,584,584]{2,3,1,0:T(8,128)} %get-tuple-element.71, f32[8,2,584]{2,1,0:T(2,128)S(1)} %multiply_divide_fusion, bf16[8,2,64,584]{3,2,1,0:T(8,128)(2,1)} %copy-done.12, bf16[8,584,2,64]{1,3,2,0:T(8,128)(2,1)S(1)} %copy-done.11), kind=kOutput, calls=%fused_computation.35 | convolution fusion | flops 725757824 | bytes 35208192 | tf_op jit(solution)/shard_map/transpose(jvp(bhqk,bkhe->bqhe))/dot_general | solution.py:22
  649.0 17.5 %fusion.10 = bf16[8,2,584,584]{2,3,1,0:T(8,128)(2,1)} fusion(f32[8,2,584,584]{2,3,1,0:T(8,128)} %get-tuple-element.71, bf16[8,2,584,584]{2,3,1,0:T(8,128)(2,1)} %get-tuple-element.74, f32[8,2,584]{2,1,0:T(2,128)S(1)} %neg.22, f32[8,2,584]{2,1,0:T(2,128)S(1)} %copy-done.25, pred[584]{0:T(1024)(128)(4,1)S(1)} %copy-done.53), kind=kLoop, calls=%fused_computation.33 | loop fusion | flops 38198272 | bytes 43730504 | tf_op jit(solution)/shard_map/transpose(jvp())/mul | solution.py:28
  666.6 8.3 fusion.93
  674.9 8.4 fusion.92
  683.4 8.4 fusion.106
  691.8 8.0 fusion.109
  699.8 17.3 %fusion.33 = bf16[8,584,1024]{2,1,0:T(8,128)(2,1)} fusion(f32[8,584,1024,1]{2,1,3,0:T(8,128)} %fusion.106, f32[8,584,1024,1]{2,1,3,0:T(8,128)} %fusion.109, bf16[8,584,2,64]{1,3,2,0:T(8,128)(2,1)S(1)} %copy-done.15, bf16[1024,2,64]{0,2,1:T(8,128)(2,1)S(1)} %copy-done.35), kind=kOutput, calls=%fused_computation.63 | convolution fusion | flops 1239089152 | bytes 49299456 | tf_op jit(solution)/shard_map/bthe,dhe->btd/dot_general | solution.py:22
  717.2 50.2 %copy.72 = bf16[8,577,5,1024]{3,0,2,1:T(8,128)(2,1)} copy(bf16[8,577,5,1024]{3,1,2,0:T(8,128)(2,1)} %bitcast.159) | data formatting | bytes 94535680
  767.4 32.7 %copy.44 = bf16[8,577,5120]{2,1,0:T(8,128)(2,1)} copy(bf16[8,577,5120]{2,0,1:T(8,128)(2,1)} %bitcast.158) | data formatting | bytes 94535680 | tf_op jit(solution)/shard_map/reshape | solution.py:58
  800.1 13.2 convert_element_type.156
  813.2 100.5 %all-reduce.11.cloned.1.call-done = (bf16[8,584,1024]{2,1,0:T(8,128)(2,1)}, bf16[8,584,1024]{2,1,0:T(8,128)(2,1)}) async-done(((bf16[8,584,1024]{2,1,0:T(8,128)(2,1)}, bf16[8,584,1024]{2,1,0:T(8,128)(2,1)}), (bf16[8,584,1024]{2,1,0:T(8,128)(2,1)}, bf16[8,584,1024]{2,1,0:T(8,128)(2,1)})) %all-reduce.11.cloned.1.call-update) | async-done | bytes 19136528 | tf_op jit(solution)/shard_map/psum | solution.py:35
  913.8 18.6 %fusion.13 = (f32[1024]{0:T(1024)}, f32[]{:T(128)}, f32[8,584,1024]{2,1,0:T(8,128)}) fusion(f32[]{:T(128)} %bitcast.13, bf16[8,577,1024]{2,1,0:T(8,128)(2,1)} %slice.42, f32[1024]{0:T(1024)S(1)} %copy-done.47, bf16[8,584,1024]{2,1,0:T(8,128)(2,1)} %get-tuple-element.55), kind=kLoop, calls=%fused_computation.40 | loop fusion | flops 33487872 | bytes 38166536 | tf_op jit(solution)/shard_map/reduce_sum | solution.py:73
  932.8 13.4 fusion.32
  946.1 38.1 %convolution_convert_fusion = bf16[8,577,4096]{2,1,0:T(8,128)(2,1)} fusion(bf16[768,4096]{1,0:T(8,128)(2,1)} %param.28, s32[]{:T(128)S(6)} %select_n.12, bf16[8,577,1024]{2,1,0:T(8,128)(2,1)} %fusion.32, bf16[8,577,5120]{2,1,0:T(8,128)(2,1)} %copy.44), kind=kOutput, calls=%fused_computation.29 | convolution fusion | flops 29074448384 | bytes 100827136 | tf_op jit(solution)/shard_map/btc,cp->btp/dot_general | solution.py:22
  984.3 13.0 convert_reduce_fusion
  997.3 31.9 %slice.43 = bf16[8,577,5120]{2,1,0:T(8,128)(2,1)} slice(bf16[8,577,6144]{2,1,0:T(8,128)(2,1)} %all-gather.2.cloned.1.call-done), slice={[0:8], [0:577], [1024:6144]} | slice | bytes 94535680 | tf_op jit(solution)/shard_map/slice | solution.py:70
  1029.2 61.7 %copy.73 = bf16[8,577,5120]{1,2,0:T(8,128)(2,1)} copy(bf16[8,577,5120]{2,1,0:T(8,128)(2,1)} %slice.43) | data formatting | bytes 94535680
  1090.9 35.6 %pad.9.clone = bf16[8,584,5120]{1,2,0:T(8,128)(2,1)} pad(bf16[8,577,5120]{1,2,0:T(8,128)(2,1)} %copy.73, bf16[]{:T(256)} %constant.99.clone.1), padding=0_0x0_7x0_0 | pad | bytes 95109120 | tf_op jit(solution)/shard_map/jit(_pad)/pad | solution.py:70
  1126.5 64.6 %copy.55 = bf16[8,584,5,1024]{3,1,2,0:T(8,128)(2,1)} copy(bf16[8,584,5,1024]{1,3,2,0:T(8,128)(2,1)} %bitcast.157) | data formatting | bytes 95682560
  1191.1 10.5 fusion.84
  1201.7 12.2 fusion.81
  1214.6 6.6 fusion.97
  1221.3 6.5 convolution_bitcast_fusion
  1233.8 10.9 fusion.23
  1244.7 11.9 fusion.31
  1257.2 17.1 %fusion.29 = bf16[8,584,1024]{2,1,0:T(8,128)(2,1)} fusion(bf16[8,584,1024]{2,1,0:T(8,128)(2,1)} %copy-done.7, bf16[8,584,1024]{2,1,0:T(8,128)(2,1)} %param.15, bf16[8,584,1024]{2,1,0:T(8,128)(2,1)} %get-tuple-element.56, f32[8,584]{1,0:T(8,128)S(1)} %negate_multiply_fusion.1, f32[8,584]{1,0:T(8,128)S(1)} %multiply_multiply_fusion.5, f32[1024]{0:T(1024)S(1)} %bitcast.165, ...), kind=kLoop, calls=%fused_computation.56 | loop fusion | flops 57409536 | bytes 38351872 | tf_op jit(solution)/shard_map/convert_element_type | solution.py:96
  1274.3 81.9 %fusion.58 = f32[768,4096]{1,0:T(8,128)} fusion(bf16[8,577,4096]{2,0,1:T(8,128)(2,1)} %param.17, s32[]{:T(128)S(6)} %select_n.12, bf16[8,577,1024]{2,1,0:T(8,128)(2,1)} %fusion.32, bf16[8,577,5120]{2,1,0:T(8,128)(2,1)} %copy.44), kind=kOutput, calls=%fused_computation.110 | convolution fusion | flops 29055541248 | bytes 107118592 | tf_op jit(solution)/shard_map/btc,btp->cp/dot_general | solution.py:22
  1356.2 5.9 add_convert_fusion.1
  (155 shorter events, 54.2 us)
Async XLA Ops:
  7.2 185.8 %copy-start = (bf16[1024,512]{1,0:T(8,128)(2,1)S(1)}, bf16[1024,512]{1,0:T(8,128)(2,1)}, u32[]{:S(2)}) copy-start(bf16[1024,512]{1,0:T(8,128)(2,1)} %param.24) | copy-start | bytes 3145732
  7.2 174.3 %all-reduce.7.cloned.1.call-start = ((), (), s32[]{:S(2)}) async-start(), calls=%async_computation.1 | async-start | bytes 19136512 | tf_op jit(solution)/shard_map/psum | solution.py:35
  7.3 6.6 copy-start.2
  7.3 26.5 %copy-start.52 = (pred[584]{0:T(1024)(128)(4,1)}, pred[584]{0:T(1024)(128)(4,1)S(1)}, u32[]{:S(2)}) copy-start(pred[584]{0:T(1024)(128)(4,1)S(1)} %iota_compare_fusion) | copy-start | bytes 1756
  8.3 8.4 copy-start.40
  8.3 184.7 %copy-start.48 = (f32[1,1024]{1,0:T(1,128)}, f32[1,1024]{1,0:T(1,128)S(1)}, u32[]{:S(2)}) copy-start(f32[1,1024]{1,0:T(1,128)S(1)} %get-tuple-element.67) | copy-start | bytes 12292
  8.3 592.8 %copy-start.42 = (f32[1,1024]{1,0:T(1,128)}, f32[1,1024]{1,0:T(1,128)S(1)}, u32[]{:S(2)}) copy-start(f32[1,1024]{1,0:T(1,128)S(1)} %get-tuple-element.64) | copy-start | bytes 12292
  13.9 7.7 copy-start.20
  21.6 8.8 copy-start.13
  21.6 8.8 copy-start.34
  33.8 24.5 %copy-start.10 = (bf16[8,584,2,64]{1,3,2,0:T(8,128)(2,1)}, bf16[8,584,2,64]{1,3,2,0:T(8,128)(2,1)S(1)}, u32[]{:S(2)}) copy-start(bf16[8,584,2,64]{1,3,2,0:T(8,128)(2,1)S(1)} %convolution_convert_fusion.10) | copy-start | bytes 3588100
  49.1 9.2 copy-start.24
  71.6 364.6 %all-gather.2.cloned.1.call-start = ((), (), s32[]{:S(2)}) async-start(), calls=%async_computation.3 | async-start | bytes 64585728 | tf_op jit(solution)/shard_map/all_gather | solution.py:67
  108.4 7.5 copy-start.51
  115.8 461.6 %all-reduce.9.cloned.1.call-start = ((), (), s32[]{:S(2)}) async-start(), calls=%async_computation.4 | async-start | bytes 19136512 | tf_op jit(solution)/shard_map/psum | solution.py:35
  190.2 13.4 copy-start.3
  190.2 410.8 %copy-start.22 = (f32[8,584]{1,0:T(8,128)}, f32[8,584]{1,0:T(8,128)S(1)}, u32[]{:S(2)}) copy-start(f32[8,584]{1,0:T(8,128)S(1)} %broadcast_multiply_fusion) | copy-start | bytes 56068
  193.0 408.1 %copy-start.36 = (f32[8,584]{1,0:T(8,128)}, f32[8,584]{1,0:T(8,128)S(1)}, u32[]{:S(2)}) copy-start(f32[8,584]{1,0:T(8,128)S(1)} %fusion.115) | copy-start | bytes 56068
  230.3 214.4 %copy-start.54 = (bf16[512,1024]{1,0:T(8,128)(2,1)S(1)}, bf16[512,1024]{1,0:T(8,128)(2,1)}, u32[]{:S(2)}) copy-start(bf16[512,1024]{1,0:T(8,128)(2,1)} %param.26) | copy-start | bytes 3145732
  470.4 443.4 %all-reduce.11.cloned.1.call-start = ((), (), s32[]{:S(2)}) async-start(), calls=%async_computation.5 | async-start | bytes 38273024 | tf_op jit(solution)/shard_map/psum | solution.py:35
  587.9 13.1 copy-start.5
  601.1 20.1 %copy-start.29 = (bf16[2,64,1024]{2,1,0:T(8,128)(2,1)S(1)}, bf16[2,64,1024]{2,1,0:T(8,128)(2,1)}, u32[]{:S(2)}) copy-start(bf16[2,64,1024]{2,1,0:T(8,128)(2,1)} %param.21) | copy-start | bytes 786436
  625.8 9.2 copy-start.11
  634.9 14.1 %copy-start.53 = (pred[584]{0:T(1024)(128)(4,1)S(1)}, pred[584]{0:T(1024)(128)(4,1)}, u32[]{:S(2)}) copy-start(pred[584]{0:T(1024)(128)(4,1)} %copy-done.52) | copy-start | bytes 1756
  674.9 8.5 copy-start.18
  674.9 8.4 copy-start.31
  683.3 8.4 copy-start.16
  683.4 8.4 copy-start.33
  691.8 8.0 copy-start.15
  691.8 8.0 copy-start.35
  717.1 639.1 %reduce-scatter.2.cloned.1.call-start = ((), (), s32[]{:S(2)}) async-start(), calls=%async_computation.2 | async-start | bytes 43057152 | tf_op jit(solution)/shard_map/reduce_scatter | solution.py:61
  800.1 113.7 %copy-start.47 = (f32[1024]{0:T(1024)S(1)}, f32[1024]{0:T(1024)}, u32[]{:S(2)}) copy-start(f32[1024]{0:T(1024)} %param.27) | copy-start | bytes 12292
  913.8 19.0 %copy-start.6 = (f32[8,584,1024]{2,1,0:T(8,128)S(1)}, f32[8,584,1024]{2,1,0:T(8,128)}, u32[]{:S(2)}) copy-start(f32[8,584,1024]{2,1,0:T(8,128)} %convert_element_type.156) | copy-start | bytes 57409540
  1191.1 10.6 copy-start.23
  1191.1 10.6 copy-start.37
  1191.1 10.6 copy-start.43
  1191.1 10.6 copy-start.49
  1201.7 12.9 copy-start.9
  1214.6 13.2 slice-start
  1214.6 13.2 slice-start.1
  1221.3 6.5 slice-start.2
  1221.3 6.5 copy-start.17
  1233.8 10.9 copy-start.39
  1233.8 10.9 copy-start.27
  1244.7 11.9 copy-start.45
  1244.7 11.9 copy-start.46
  1274.3 81.9 %copy-start.44 = (f32[4096]{0:T(1024)S(1)}, f32[4096]{0:T(1024)}, u32[]{:S(2)}) copy-start(f32[4096]{0:T(1024)} %param.29) | copy-start | bytes 49156
  1274.3 87.8 %copy-start.1 = (bf16[1024,512]{1,0:T(8,128)(2,1)S(1)}, bf16[1024,512]{1,0:T(8,128)(2,1)}, u32[]{:S(2)}) copy-start(bf16[1024,512]{1,0:T(8,128)(2,1)} %param.24) | copy-start | bytes 3145732
  (16 other events, 47.3 us)
Sparse Core Ops, SparseCore 0:
  71.7 109.8 all-reduce.6
  183.1 252.9 all-gather.1
  470.5 106.8 all-reduce.8
  717.2 196.4 all-reduce.10
  984.4 188.4 reduce-scatter.1
where the time goes:
time: 1380 us; the launch traced here: 1370 us
  waiting for transfers between devices  467 us (34%)
  matrix products  353 us (26%)
  local copies, waits for them, and re-layouts  313 us (23%)
  other arithmetic  219 us (16%)
  between operations  17.4 us (1%)
    dot_general x26, matrix products, matmul(): jnp.einsum(eq_form, lhs_in, rhs_in, preferred_element_type=jnp.float32)  338 us
    psum x3, waiting for transfers between devices, group_sum(): return lax.psum(part_sum.astype(jnp.bfloat16), 'tp').astype(jnp.float32)  261 us
    all_gather x1, waiting for transfers between devices, local_step(): grad_feats = lax.all_gather(grad_feats_local, 'tp', axis=2, tiled=True)  206 us
    unnamed x121, local copies, waits for them, and re-layouts  195 us
    reduce_sum x4, other arithmetic, layer_norm(): centred * lax.rsqrt(row_var + LN_EPS) * ln_gain + ln_bias  46.3 us
    pad x1, local copies, waits for them, and re-layouts, local_step(): jnp.pad(grad_feats[:, :, width:], pad_rows).reshape(inter_feats.shape)  35.6 us
    reshape x1, local copies, waits for them, and re-layouts, local_step(): inter_feats[:, :real_rows].reshape(tile_count, real_rows, -1)  32.7 us
    slice x1, local copies, waits for them, and re-layouts, local_step(): grad_feats[:, :, width:]  31.9 us
  transfers between devices with their start and end apart: 5, of which 4 were waited for; matrix products, arithmetic and copies ran while one was open for 41% of the time, Pallas kernels for 0%

commit v1 on v0

v1 whole, which is shorter than its diff:
```python
import functools
import math
import jax
import jax.numpy as jnp
from jax import lax
from jax.experimental import pallas as pl
from jax.experimental.layout import Layout, with_layout_constraint
from jax.experimental.pallas import tpu as pltpu
from jax.sharding import PartitionSpec as P

LN_EPS = 1e-5


def layer_norm(values, ln_gain, ln_bias):
    row_mean = jnp.mean(values, axis=-1, keepdims=True)
    centred = values - row_mean
    row_var = jnp.mean(centred * centred, axis=-1, keepdims=True)
    return (centred * lax.rsqrt(row_var + LN_EPS) * ln_gain + ln_bias).astype(jnp.bfloat16)


def gelu_bf16(pre_act):
    return jax.nn.gelu(pre_act, approximate=False).astype(jnp.bfloat16)


def matmul(eq_form, lhs_in, rhs_in):
    return jnp.einsum(eq_form, lhs_in, rhs_in, preferred_element_type=jnp.float32)


def after(value, earlier):
    return lax.optimization_barrier((value, earlier))


def attend(real_rows, q_act, k_act, v_act):
    tokens = q_act.shape[0]
    score_scale = q_act.shape[2] ** -0.5
    scores = matmul('qhe,khe->hqk', q_act, k_act) * score_scale
    key_ok = (jnp.arange(tokens) < real_rows)[None, None, :]
    attn_probs = jax.nn.softmax(jnp.where(key_ok, scores, -1e30), axis=-1).astype(jnp.bfloat16)
    return matmul('hqk,khe->qhe', attn_probs, v_act).astype(jnp.bfloat16)


def feats_kernel(blocks, piece, real_rows, grad_ref, rows_ref, *rest):
    out_ref, held, sems = rest[-3:]
    tokens = held.shape[2]
    tile = pl.program_id(0)
    tiles = pl.num_programs(0)
    slot = lax.rem(tile, 2)

    def copies(at_tile, at_slot):
        return [pltpu.make_async_copy(held.at[at_slot, n],
                                      out_ref.at[at_tile, feat, :, pl.ds(col * piece, piece)],
                                      sems.at[at_slot, n])
                for n, (_, feat, col) in enumerate(blocks)]

    @pl.when(tile >= 2)
    def _():
        for copy in copies(tile - 2, slot):
            copy.wait()

    is_real = lax.broadcasted_iota(jnp.int32, (tokens, piece), 0) < real_rows
    out_now = copies(tile, slot)
    for n, (row, _, _) in enumerate(blocks):
        block = lax.dot_general(grad_ref[0], rows_ref[pl.ds(row * piece, piece), :],
                                (((1,), (1,)), ((), ())), preferred_element_type=jnp.float32)
        held[slot, n] = jnp.where(is_real, block, 0.0).astype(jnp.bfloat16)
        out_now[n].start()

    @pl.when(tile == tiles - 1)
    def _():
        for copy in copies(tile - 1, 1 - slot) + out_now:
            copy.wait()


def grad_feats_part(grad, rows, blocks, piece, feats, tokens, width, prior):
    tiles, real_rows, depth = grad.shape
    flops = 2 * tiles * tokens * depth * piece * len(blocks)
    in_specs = [pl.BlockSpec((1, tokens, depth), lambda b: (b, 0, 0)),
                pl.BlockSpec(rows.shape, lambda b: (0, 0), pipeline_mode=pl.Buffered(1))]
    args = [grad, rows]
    aliases = {}
    if prior is not None:
        in_specs.append(pl.BlockSpec(memory_space=pl.ANY))
        args.append(prior)
        aliases = {2: 0}
    return pl.pallas_call(
        functools.partial(feats_kernel, blocks, piece, real_rows),
        grid=(tiles,),
        out_shape=jax.ShapeDtypeStruct((tiles, feats, tokens, width), jnp.bfloat16),
        in_specs=in_specs,
        out_specs=pl.BlockSpec(memory_space=pl.ANY),
        scratch_shapes=[pltpu.VMEM((2, len(blocks), tokens, piece), jnp.bfloat16),
                        pltpu.SemaphoreType.DMA((2, len(blocks)))],
        input_output_aliases=aliases,
        compiler_params=pltpu.CompilerParams(dimension_semantics=("arbitrary",), vmem_limit_bytes=58 * 1024 * 1024),
        cost_estimate=pl.CostEstimate(flops=flops, bytes_accessed=2 * (grad.size + rows.size + tiles * tokens * piece * len(blocks)), transcendentals=0),
    )(*args)


def rows_grad_kernel(real_rows, step, feats_ref, grad_ref, out_ref):
    tile = pl.program_id(0)
    tokens, depth = grad_ref.shape[1:]

    @pl.when(tile == 0)
    def _():
        out_ref[...] = jnp.zeros_like(out_ref)

    is_real = lax.broadcasted_iota(jnp.int32, (tokens, step), 0) < real_rows
    turned = feats_ref[0].T
    for at in range(0, depth, step):
        cols = pl.ds(at, step)
        grad = jnp.where(is_real, grad_ref[0, :, cols], jnp.bfloat16(0))
        out_ref[:, cols] += jnp.dot(turned, grad, preferred_element_type=jnp.float32)


def rows_grad(feats_local, grad):
    tiles, tokens, local = feats_local.shape
    real_rows, depth = grad.shape[1:]
    return pl.pallas_call(
        functools.partial(rows_grad_kernel, real_rows, min(512, depth)),
        grid=(tiles,),
        out_shape=jax.ShapeDtypeStruct((local, depth), jnp.float32),
        in_specs=[pl.BlockSpec((1, tokens, local), lambda b: (b, 0, 0)),
                  pl.BlockSpec((1, tokens, depth), lambda b: (b, 0, 0))],
        out_specs=pl.BlockSpec((local, depth), lambda b: (0, 0)),
        compiler_params=pltpu.CompilerParams(dimension_semantics=("arbitrary",), vmem_limit_bytes=58 * 1024 * 1024),
        cost_estimate=pl.CostEstimate(flops=2 * tiles * tokens * local * depth, bytes_accessed=2 * (feats_local.size + grad.size) + 4 * local * depth, transcendentals=0),
    )(feats_local, grad)


def local_step(hidden, inter_feats, proj_grad, w_query, w_key, w_value, w_out, ln_params, gate_params, w_fc1, b_fc1, w_fc2, b_fc2, w_proj, b_proj):
    tile_count, tokens, width = hidden.shape
    real_rows = proj_grad.shape[1]
    feats = inter_feats.shape[2]
    feat_local, proj_dim = w_proj.shape
    local_heads, head_dim = w_query.shape[1:]
    local_width = local_heads * head_dim
    group = lax.axis_size('tp')
    heads = group * local_heads
    mine = lax.axis_index('tp')
    piece = math.gcd(feat_local, width)
    per_dev, per_feat = feat_local // piece, width // piece

    flip = lambda w: w.reshape(width, local_width).T
    w_attn = lax.all_gather(jnp.stack([flip(w_query), flip(w_key), flip(w_value), w_out.reshape(local_width, width)]), 'tp', axis=1, tiled=True)
    fc1 = lax.all_gather(w_fc1, 'tp', axis=1, tiled=True)
    bias1 = lax.all_gather(b_fc1, 'tp', axis=0, tiled=True)
    fc2 = lax.all_gather(w_fc2, 'tp', axis=0, tiled=True)
    gather_rows = lambda part: lax.all_gather(part, 'tp', axis=0, tiled=True)
    w_parts = [w_proj[j * piece:(j + 1) * piece] for j in range(per_dev)]

    x_wide = lax.dynamic_index_in_dim(hidden, mine, 0, keepdims=False).astype(jnp.float32)
    normed, norm1_pull = jax.vjp(layer_norm, x_wide, ln_params[0], ln_params[1])
    proj_grad = with_layout_constraint(proj_grad, Layout((0, 1, 2)))
    normed, (proj_grad, w_parts[0]) = after(normed, (proj_grad, w_parts[0]))
    proj_rows = [gather_rows(w_parts[0])]
    w_qkv = w_attn[:3].reshape(3 * width, width)
    qkv = matmul('td,jd->tj', normed, w_qkv).astype(jnp.bfloat16).reshape(tokens, 3, heads, head_dim)
    context, attend_pull = jax.vjp(functools.partial(attend, real_rows), qkv[:, 0], qkv[:, 1], qkv[:, 2])
    context = context.reshape(tokens, width)
    attn_out = matmul('tj,jd->td', context, w_attn[3])
    gate_attn = jnp.tanh(gate_params[0])
    gate_mlp = jnp.tanh(gate_params[1])
    x_one_wide = (x_wide + gate_attn * attn_out).astype(jnp.bfloat16).astype(jnp.float32)
    normed_two, norm2_pull = jax.vjp(layer_norm, x_one_wide, ln_params[2], ln_params[3])
    pre_act = matmul('td,df->tf', normed_two, fc1) + bias1
    mlp_act, gelu_pull = jax.vjp(gelu_bf16, pre_act)
    mlp_out = matmul('tf,fd->td', mlp_act, fc2) + b_fc2
    x_two = (x_one_wide + gate_mlp * mlp_out).astype(jnp.bfloat16)

    inter = jnp.transpose(inter_feats, (0, 2, 1, 3))
    grad_mine = lax.dynamic_index_in_dim(proj_grad, mine, 0, keepdims=False)

    def feats_part(j, prior):
        blocks = []
        for d in range(group):
            at = d * per_dev + j
            if at >= per_feat:
                blocks.append((d, at // per_feat - 1, at % per_feat))
        return grad_feats_part(proj_grad, proj_rows[j], tuple(blocks), piece, feats, tokens, width, prior)

    w_parts[1], x_two = after(w_parts[1], x_two)
    x_two_all = lax.all_gather(x_two, 'tp', axis=0, tiled=False)
    proj_rows.append(gather_rows(w_parts[1]))
    proj_rows[0], x_two = after(proj_rows[0], x_two)
    for part in w_parts[2:]:
        part, proj_rows[0] = after(part, proj_rows[0])
        proj_rows.append(gather_rows(part))
    grad_inter = feats_part(0, None)
    x_two_all, grad_inter = after(x_two_all, grad_inter)

    cols = []
    for j in range(per_dev):
        at = mine * per_dev + j
        feat, col = at // per_feat, (at % per_feat) * piece
        from_two = lax.dynamic_slice_in_dim(x_two_all, col, piece, axis=2)
        from_inter = lax.dynamic_slice(inter, (0, jnp.maximum(feat - 1, 0), 0, col), (tile_count, 1, tokens, piece))[:, 0]
        cols.append(jnp.where(feat == 0, from_two, from_inter))
    feats_local = jnp.concatenate(cols, axis=-1)
    grad_w_proj = rows_grad(feats_local, proj_grad)
    for j in range(1, per_dev - 1):
        proj_rows[j], grad_w_proj = after(proj_rows[j], grad_w_proj)
        grad_inter = feats_part(j, grad_inter)
    proj_rows[-1], grad_inter = after(proj_rows[-1], grad_inter)

    rows_two = jnp.concatenate([proj_rows[at % per_dev][(at // per_dev) * piece:(at // per_dev + 1) * piece] for at in range(per_feat)], axis=0)
    grad_x_two = matmul('tp,cp->tc', grad_mine, rows_two).astype(jnp.bfloat16)
    grad_x_two = jnp.pad(grad_x_two, ((0, tokens - real_rows), (0, 0))).astype(jnp.float32)
    grad_mlp = gate_mlp * grad_x_two
    grad_gate_mlp = jnp.sum(grad_x_two * mlp_out) * (1.0 - gate_mlp * gate_mlp)
    grad_b_fc2 = jnp.sum(grad_mlp, axis=0)
    grad_mlp_low = grad_mlp.astype(jnp.bfloat16)
    grad_fc2 = matmul('tf,td->fd', mlp_act, grad_mlp_low).astype(jnp.bfloat16)
    grad_act = matmul('td,fd->tf', grad_mlp_low, fc2).astype(jnp.bfloat16)
    grad_pre = gelu_pull(grad_act)[0]
    grad_b_fc1 = jnp.sum(grad_pre, axis=0)
    grad_pre_low = grad_pre.astype(jnp.bfloat16)
    grad_fc1 = matmul('tf,td->fd', grad_pre_low, normed_two).astype(jnp.bfloat16)
    grad_normed_two = matmul('tf,df->td', grad_pre_low, fc1).astype(jnp.bfloat16)
    grad_normed_two, (grad_fc1, grad_fc2) = after(grad_normed_two, (grad_fc1, grad_fc2))
    grad_w_fc2 = lax.psum_scatter(grad_fc2, 'tp', scatter_dimension=0, tiled=True)
    grad_w_fc1 = lax.psum_scatter(grad_fc1, 'tp', scatter_dimension=0, tiled=True)
    grad_x_ln_two, grad_gain_two, grad_bias_two = norm2_pull(grad_normed_two)
    grad_x_one = (grad_x_two + grad_x_ln_two).astype(jnp.bfloat16).astype(jnp.float32)
    grad_attn = gate_attn * grad_x_one
    grad_gate_attn = jnp.sum(grad_x_one * attn_out) * (1.0 - gate_attn * gate_attn)
    grad_attn_low = grad_attn.astype(jnp.bfloat16)
    grad_wo = matmul('tj,td->jd', context, grad_attn_low)
    grad_context = matmul('td,jd->tj', grad_attn_low, w_attn[3]).astype(jnp.bfloat16).reshape(tokens, heads, head_dim)
    grad_qkv = jnp.stack(attend_pull(grad_context), axis=1).reshape(tokens, 3 * width)
    grad_wqkv = matmul('tj,td->jd', grad_qkv, normed).reshape(3, width, width)
    grad_w_attn = jnp.concatenate([grad_wqkv, grad_wo[None]]).astype(jnp.bfloat16)
    grad_w_attn = lax.psum_scatter(grad_w_attn, 'tp', scatter_dimension=1, tiled=True).astype(jnp.float32)
    unflip = lambda g: g.T.reshape(width, local_heads, head_dim)
    grad_normed = matmul('tj,jd->td', grad_qkv, w_qkv).astype(jnp.bfloat16)
    grad_x_ln, grad_gain, grad_bias = norm1_pull(grad_normed)
    grad_tile = (grad_x_one + grad_x_ln).astype(jnp.bfloat16)

    proj_rows[-1], grad_tile = after(proj_rows[-1], grad_tile)
    grad_tile, (grad_w_fc1, grad_w_fc2) = after(grad_tile, (grad_w_fc1, grad_w_fc2))
    grad_hidden = lax.all_gather(grad_tile, 'tp', axis=0, tiled=False)
    grad_w_fc1, grad_w_fc2 = grad_w_fc1.astype(jnp.float32).T, grad_w_fc2.astype(jnp.float32)
    grad_inter = jnp.transpose(feats_part(per_dev - 1, grad_inter), (0, 2, 1, 3))
    inter_mine = lax.dynamic_index_in_dim(inter, mine, 0, keepdims=False)
    feats_mine = jnp.concatenate([x_two[None], inter_mine], axis=0)[:, :real_rows]
    proj_sum = b_proj
    for j in range(per_dev):
        part = jnp.concatenate([feats_mine[at // per_feat, :, (at % per_feat) * piece:(at % per_feat + 1) * piece]
                                for at in range(j, group * per_dev, per_dev)], axis=-1)
        proj_sum = proj_sum + matmul('tc,cp->tp', part, proj_rows[j])
    proj_out = proj_sum.astype(jnp.bfloat16)[None]

    grad_b_proj = jnp.sum(grad_mine, axis=0, dtype=jnp.float32)
    small = [grad_gain, grad_bias, grad_gain_two, grad_bias_two, grad_b_fc2, grad_b_fc1, grad_b_proj, jnp.stack([grad_gate_attn, grad_gate_mlp])]
    sums = lax.psum(jnp.concatenate(small), 'tp')
    ends = [sum(s.shape[0] for s in small[:n + 1]) for n in range(len(small))]
    grad_gain, grad_bias, grad_gain_two, grad_bias_two, grad_b_fc2, grad_b_fc1, grad_b_proj, grad_gates = jnp.split(sums, ends[:-1])
    grad_ln = jnp.stack([grad_gain, grad_bias, grad_gain_two, grad_bias_two])
    grad_b_fc1 = lax.dynamic_slice_in_dim(grad_b_fc1, mine * b_fc1.shape[0], b_fc1.shape[0], axis=0)
    return (proj_out, grad_hidden, grad_inter, unflip(grad_w_attn[0]), unflip(grad_w_attn[1]), unflip(grad_w_attn[2]), grad_w_attn[3].reshape(local_heads, head_dim, width), grad_ln, grad_gates, grad_w_fc1, grad_b_fc1, grad_w_fc2, grad_b_fc2, grad_w_proj, grad_b_proj)


def solution(mesh):
    tiles_spec = P('dp', None, None)
    inter_spec = P('dp', None, None, None)
    head_cols = P(None, 'tp', None)
    in_specs = (tiles_spec, inter_spec, tiles_spec, head_cols, head_cols, head_cols, P('tp', None, None), P(None, None), P(None), P(None, 'tp'), P('tp'), P('tp', None), P(None), P('tp', None), P(None))
    grad_heads = P('dp', 'tp', None)
    out_specs = (P(('dp', 'tp'), None, None), tiles_spec, inter_spec, grad_heads, grad_heads, grad_heads, P(('dp', 'tp'), None, None), P('dp', None), P('dp'), P('dp', 'tp'), P(('dp', 'tp')), P(('dp', 'tp'), None), P('dp'), P(('dp', 'tp'), None), P('dp'))
    return jax.shard_map(local_step, mesh=mesh, in_specs=in_specs, out_specs=out_specs, check_vma=False)
```

time: 1380 us -> 822 us (0.60)
  waiting for transfers between devices: 467 us -> 36.2 us
  Pallas kernels: 0 us -> 281 us
  local copies, waits for them, and re-layouts: 313 us -> 96.9 us
  other arithmetic: 219 us -> 98.4 us
  matrix products: 353 us -> 234 us
  blocking collectives: 0 us -> 51.6 us
    pallas_call x0 -> x4, Pallas kernels: none -> 281 us  [the longest x3 232 us: grad_feats_part(): pl.pallas_call(functools.partial(feats_kernel, blocks, piece, real_rows),...]
    psum x3 -> x0, waiting for transfers between devices: 261 us -> none  [group_sum(): return lax.psum(part_sum.astype(jnp.bfloat16), 'tp').astype(jnp.float32)]
    all_gather x1 -> x8, waiting for transfers between devices: 206 us -> 33.1 us  [the longest x3 33.1 us: local_step(): gather_rows = lambda part: lax.all_gather(part, 'tp', axis=0, tiled=True)]
    unnamed x121 -> x135, local copies, waits for them, and re-layouts: 195 us -> 62.7 us
    dot_general x26 -> x22, matrix products: 338 us -> 234 us  [matmul(): jnp.einsum(eq_form, lhs_in, rhs_in, preferred_element_type=jnp.float32)]
    convert_element_type x5 -> x2, other arithmetic: 72.5 us -> 4.88 us  [the longest x1 3.32 us: local_step(): grad_tile = (grad_x_one + grad_x_ln).astype(jnp.bfloat16)]
    reduce_sum x4 -> x3, other arithmetic: 46.3 us -> 4.91 us  [layer_norm(): centred * lax.rsqrt(row_var + LN_EPS) * ln_gain + ln_bias]
    reduce_sum x3 -> x2, other arithmetic: 48.1 us -> 7.59 us  [the longest x1 4.03 us: local_step(): grad_gate_mlp = jnp.sum(grad_x_two * mlp_out) * (1.0 - gate_mlp * gate_mlp)]
  transfers between devices with their start and end apart: 5 -> 11, of which waited for: 4 -> 3; matrix products, arithmetic and copies ran while one was open for 41% -> 42% of each run, Pallas kernels for 0% -> 34%
where the time goes in v1:
time: 822 us; the launch traced here: 817 us
  Pallas kernels  281 us (34%)
  matrix products  234 us (28%)
  other arithmetic  98.4 us (12%)
  local copies, waits for them, and re-layouts  96.9 us (12%)
  blocking collectives  51.6 us (6%)
  waiting for transfers between devices  36.2 us (4%)
  between operations  17.8 us (2%)
    dot_general x22, matrix products, matmul(): jnp.einsum(eq_form, lhs_in, rhs_in, preferred_element_type=jnp.float32)  234 us
    pallas_call x3, Pallas kernels, grad_feats_part(): pl.pallas_call(functools.partial(feats_kernel, blocks, piece, real_rows),...  232 us
    unnamed x135, local copies, waits for them, and re-layouts  62.7 us
    pallas_call x1, Pallas kernels, rows_grad(): pl.pallas_call(functools.partial(rows_grad_kernel, real_rows, min(512, de...  48.9 us
    all_gather x3, waiting for transfers between devices, local_step(): gather_rows = lambda part: lax.all_gather(part, 'tp', axis=0, tiled=True)  33.1 us
    sub x1, other arithmetic, attend(): jax.nn.softmax(jnp.where(key_ok, scores, -1e+30), axis=-1)  27.3 us
    psum x1, blocking collectives, local_step(): sums = lax.psum(jnp.concatenate(small), 'tp')  26.8 us
    all_gather x1, blocking collectives, local_step(): bias1 = lax.all_gather(b_fc1, 'tp', axis=0, tiled=True)  24.9 us
  transfers between devices with their start and end apart: 11, of which 3 were waited for; matrix products, arithmetic and copies ran while one was open for 42% of the time, Pallas kernels for 34%

profile of v1, /device:TPU:112, one launch (start us, length us, event | category | flops | bytes accessed | tf_op | source)
XLA Modules:
  0.0 817.4 jit_solution(3992255375589920529)
XLA Ops:
  11.3 33.9 %copy.51.grad_ref = bf16[8,577,4096]{2,1,0:T(8,128)(2,1)} copy(bf16[8,577,4096]{2,0,1:T(8,128)(2,1)} %param.17) | data formatting | bytes 75628544 | tf_op args[2]
  51.0 6.2 fusion.133
  59.3 24.9 %all-gather.2 = f32[8,1,512]{2,1,0:T(1,128)S(1)} all-gather(f32[1,1,512]{2,1,0:T(1,128)S(1)} %bitcast.329), channel_id=1, replica_groups=mesh['dp'=2,'tp'=8] {'tp'}, dimensions={0}, use_global_device_ids=true | all-gather | bytes 18432 | tf_op jit(solution)/shard_map/all_gather | solution.py:146
  84.2 3.5 slice.234
  87.8 2.7 copy-done.5
  90.5 5.4 convolution_convert_fusion.4
  95.9 6.1 copy.52
  102.0 14.2 %fusion.87 = f32[16,584,584]{1,2,0:T(8,128)} fusion(bf16[584,3,16,64]{0,3,2,1:T(8,128)(2,1)} %bitcast.282), kind=kOutput, calls=%fused_computation.143 | convolution fusion | flops 698482688 | bytes 24449024 | tf_op jit(solution)/shard_map/jvp(qhe,khe->hqk)/dot_general | solution.py:26
  116.2 27.3 %fusion.139 = (f32[16,584]{1,0:T(8,128)S(1)}, f32[16,584,584]{1,2,0:T(8,128)}) fusion(f32[16,584,584]{1,2,0:T(8,128)} %fusion.87, pred[584]{0:T(1024)(128)(4,1)S(1)} %iota_compare_fusion), kind=kOutput, calls=%fused_computation.222 | output fusion | flops 32741960 | bytes 43693128 | tf_op jit(solution)/shard_map/jvp()/sub | solution.py:38
  144.1 9.5 %divide_convert_fusion = bf16[16,584,584]{1,2,0:T(8,128)(2,1)S(1)} fusion(f32[16,584,584]{1,2,0:T(8,128)} %get-tuple-element.173, f32[16,584]{1,0:T(8,128)S(1)} %get-tuple-element.172), kind=kLoop, calls=%fused_computation.9 | loop fusion | flops 10913792 | bytes 32778752 | tf_op jit(solution)/shard_map/jvp()/convert_element_type | solution.py:38
  158.0 5.3 convert_reduce_fusion.3
  164.5 31.4 %multiply_convert_fusion = (bf16[584,4096]{1,0:T(8,128)(2,1)}, f32[584,4096]{1,0:T(8,128)}, f32[584,4096]{1,0:T(8,128)}) fusion(f32[4096]{0:T(1024)S(1)} %bitcast.321, bf16[1024,4096]{1,0:T(8,128)(2,1)} %all-gather.16.cloned.1.call-done, bf16[584,1024]{1,0:T(8,128)(2,1)S(1)} %get-tuple-element.121, f32[1024]{0:T(1024)S(1)} %bitcast.327, ...), kind=kOutput, calls=%fused_computation.28 | convolution fusion | flops 5060411392 | bytes 33534528 | tf_op jit(solution)/shard_map/td,df->tf/dot_general | solution.py:26
  195.9 10.3 %fusion.59 = (bf16[584,1024]{1,0:T(8,128)(2,1)}, f32[584,1024]{1,0:T(8,128)}) fusion(bf16[584,1024]{1,0:T(8,128)(2,1)S(1)} %get-tuple-element.121, f32[1024]{0:T(1024)S(1)} %copy-done.47, f32[]{:T(128)} %bitcast.22, bf16[584,4096]{1,0:T(8,128)(2,1)} %get-tuple-element.118, bf16[4096,1024]{1,0:T(8,128)(2,1)} %all-gather.18.cloned.1.call-done), kind=kOutput, calls=%fused_computation.107 | convolution fusion | flops 4901937152 | bytes 17960964 | tf_op jit(solution)/shard_map/tf,fd->td/dot_general | solution.py:26
  207.1 29.4 %all-gather.12.cloned.1.call-done.rows_ref = bf16[2048,4096]{1,0:T(8,128)(2,1)} async-done(((bf16[256,4096]{1,0:T(8,128)(2,1)}), bf16[2048,4096]{1,0:T(8,128)(2,1)}) %all-gather.12.cloned.1.call-update) | async-done | bytes 16777232 | tf_op jit(solution)/shard_map/all_gather | solution.py:148
  236.8 4.7 fusion.132
  241.5 70.5 %shard_map.262.rest_0_ = bf16[8,5,584,1024]{3,2,1,0:T(8,128)(2,1)} custom-call(bf16[8,577,4096]{2,1,0:T(8,128)(2,1)} %copy.51.grad_ref, bf16[2048,4096]{1,0:T(8,128)(2,1)} %all-gather.12.cloned.1.call-done.rows_ref), custom_call_target="tpu_custom_call" | custom-call | flops 58787364864 | bytes 68943872 | tf_op jit(solution)/shard_map/pallas_call | solution.py:85
  312.0 6.9 bitcast_select_fusion.2
  318.8 3.3 pad_maximum_fusion.1.feats_ref
  322.1 48.9 %shard_map.263 = f32[768,4096]{1,0:T(8,128)} custom-call(bf16[8,584,768]{2,1,0:T(8,128)(2,1)} %pad_maximum_fusion.1.feats_ref, bf16[8,577,4096]{2,1,0:T(8,128)(2,1)} %copy.51.grad_ref), custom_call_target="tpu_custom_call" | custom-call | flops 29393682432 | bytes 57573376 | tf_op jit(solution)/shard_map/pallas_call | solution.py:118
  371.8 81.0 %shard_map.264.rest_0_ = bf16[8,5,584,1024]{3,2,1,0:T(8,128)(2,1)} custom-call(bf16[8,577,4096]{2,1,0:T(8,128)(2,1)} %copy.51.grad_ref, bf16[2048,4096]{1,0:T(8,128)(2,1)} %all-gather.20.cloned.1.call-done.rows_ref, bf16[8,5,584,1024]{3,2,1,0:T(8,128)(2,1)} %shard_map.262.rest_0_), custom_call_target="tpu_custom_call", output_to_operand_aliasing={{}: (2, {})} | custom-call | flops 68585259008 | bytes 71335936 | tf_op jit(solution)/shard_map/pallas_call | solution.py:85
  452.8 2.9 all-gather.22.cloned.1.call-done.rows_ref
  457.3 10.4 %fusion.76 = bf16[577,1024]{1,0:T(8,128)(2,1)S(1)} fusion(bf16[256,4096]{1,0:T(8,128)(2,1)} %get-tuple-element.126, bf16[256,4096]{1,0:T(8,128)(2,1)S(1)} %slice-done.7, bf16[256,4096]{1,0:T(8,128)(2,1)S(1)} %slice-done.6, bf16[256,4096]{1,0:T(8,128)(2,1)} %get-tuple-element.125, bf16[8,577,4096]{2,1,0:T(8,128)(2,1)} %copy.51.grad_ref, s32[]{:T(128)S(6)} %select_n.79), kind=kOutput, calls=%fused_computation.132 | convolution fusion | flops 4874372096 | bytes 14354436 | tf_op jit(solution)/shard_map/tp,cp->tc/dot_general | solution.py:26
  467.7 11.8 %convolution_convert_fusion = bf16[4096,1024]{1,0:T(8,128)(2,1)} fusion(bf16[584,4096]{1,0:T(8,128)(2,1)} %get-tuple-element.118, f32[]{:T(128)} %bitcast.22, bf16[577,1024]{1,0:T(8,128)(2,1)S(1)} %fusion.76), kind=kOutput, calls=%fused_computation.51 | convolution fusion | flops 4904935424 | bytes 14354436 | tf_op jit(solution)/shard_map/tf,td->fd/dot_general | solution.py:26
  479.6 17.1 %fusion.140 = (f32[4096]{0:T(1024)}, bf16[584,4096]{1,0:T(8,128)(2,1)}) fusion(f32[584,4096]{1,0:T(8,128)} %get-tuple-element.119, bf16[4096,1024]{1,0:T(8,128)(2,1)} %all-gather.18.cloned.1.call-done, f32[]{:T(128)} %bitcast.22, bf16[577,1024]{1,0:T(8,128)(2,1)S(1)} %fusion.76, f32[584,4096]{1,0:T(8,128)} %get-tuple-element.175, f32[4096]{0:T(1024)S(1)} %bitcast.322), kind=kOutput, calls=%fused_computation.223 | convolution fusion | flops 4943794176 | bytes 33523716 | tf_op jit(solution)/shard_map/td,fd->tf/dot_general | solution.py:26
  496.7 12.0 %convolution_convert_fusion.1 = bf16[4096,1024]{1,0:T(8,128)(2,1)} fusion(bf16[584,4096]{1,0:T(8,128)(2,1)} %get-tuple-element.182, bf16[584,1024]{1,0:T(8,128)(2,1)S(1)} %copy-done.4, f32[1024]{0:T(1024)S(1)} %bitcast.328, f32[1024]{0:T(1024)S(1)} %bitcast.312, f32[584]{0:T(1024)S(1)} %copy-done.38, f32[584]{0:T(1024)S(1)} %copy-done.24), kind=kOutput, calls=%fused_computation.52 | convolution fusion | flops 4906729472 | bytes 14381632 | tf_op jit(solution)/shard_map/tf,td->fd/dot_general | solution.py:26
  508.7 9.2 %fusion.72 = bf16[584,1024]{1,0:T(8,128)(2,1)S(1)} fusion(bf16[1024,4096]{1,0:T(8,128)(2,1)} %all-gather.16.cloned.1.call-done, bf16[584,4096]{1,0:T(8,128)(2,1)} %get-tuple-element.182), kind=kOutput, calls=%fused_computation.130 | convolution fusion | flops 4899545088 | bytes 14368768 | tf_op jit(solution)/shard_map/tf,df->td/dot_general | solution.py:26
  521.3 4.0 fusion.61
  526.3 3.0 fusion.75
  530.1 13.9 %fusion.6 = (f32[16,584]{1,0:T(8,128)S(1)}, bf16[16,584,584]{1,2,0:T(8,128)(2,1)}) fusion(f32[16,584,584]{1,2,0:T(8,128)} %get-tuple-element.173, f32[16,584]{1,0:T(8,128)S(1)} %multiply_divide_fusion, bf16[16,64,584]{2,1,0:T(8,128)(2,1)S(1)} %bitcast.287, bf16[584,3,16,64]{0,3,2,1:T(8,128)(2,1)} %bitcast.283), kind=kOutput, calls=%fused_computation.8 | convolution fusion | flops 725757824 | bytes 37415936 | tf_op jit(solution)/shard_map/transpose(jvp(hqk,khe->qhe))/dot_general | solution.py:26
  544.0 8.0 fusion.83
  552.1 17.7 %fusion.4 = bf16[16,584,584]{1,2,0:T(8,128)(2,1)} fusion(f32[16,584,584]{1,2,0:T(8,128)} %get-tuple-element.173, bf16[16,584,584]{1,2,0:T(8,128)(2,1)} %get-tuple-element.179, f32[16,584]{1,0:T(8,128)S(1)} %neg.22, f32[16,584]{1,0:T(8,128)S(1)} %copy-done.22, pred[584]{0:T(1024)(128)(4,1)S(1)} %copy-done.54), kind=kLoop, calls=%fused_computation.6 | loop fusion | flops 38198272 | bytes 43730504 | tf_op jit(solution)/shard_map/transpose(jvp())/mul | solution.py:36
  569.8 6.9 fusion.84
  576.7 9.4 %fusion.85 = bf16[584,1,16,64]{0,3,2,1:T(8,128)(2,1)} fusion(bf16[16,584,584]{1,2,0:T(8,128)(2,1)} %fusion.4, bf16[584,3,16,64]{0,3,2,1:T(8,128)(2,1)} %bitcast.285), kind=kOutput, calls=%fused_computation.138 | convolution fusion | flops 698482688 | bytes 14467072 | tf_op jit(solution)/shard_map/transpose(jvp(qhe,khe->hqk))/dot_general | solution.py:26
  588.2 3.1 convert_bitcast_fusion.2
  591.3 5.3 convolution_convert_fusion.5
  596.6 5.5 pad_maximum_fusion
  602.4 3.6 convert_reduce_fusion
  606.0 3.6 dynamic-slice_bitcast_fusion
  615.4 6.5 convert_reduce_fusion.1
  622.0 2.7 fusion.66
  624.7 3.3 fusion.64
  634.7 16.8 %fusion.141 = f32[577,4096]{1,0:T(8,128)} fusion(bf16[577,2048]{1,0:T(8,128)(2,1)} %get-tuple-element.130, bf16[2048,4096]{1,0:T(8,128)(2,1)} %all-gather.12.cloned.1.call-done.rows_ref), kind=kOutput, calls=%fused_computation.224 | convolution fusion | flops 9680453632 | bytes 28594176 | tf_op jit(solution)/shard_map/tc,cp->tp/dot_general | solution.py:26
  651.5 12.4 %fusion.142 = f32[577,4096]{1,0:T(8,128)} fusion(bf16[577,2048]{1,0:T(8,128)(2,1)S(1)} %copy-done.35, bf16[2048,4096]{1,0:T(8,128)(2,1)S(1)} %bitcast.302), kind=kOutput, calls=%fused_computation.225 | convolution fusion | flops 9680453632 | bytes 28594176 | tf_op jit(solution)/shard_map/tc,cp->tp/dot_general | solution.py:26
  665.4 26.8 %psum.7 = f32[13314]{0:T(1024)S(1)} all-reduce(f32[13314]{0:T(1024)S(1)} %concatenate.29), channel_id=1, replica_groups=mesh['dp'=2,'tp'=8] {'tp'}, use_global_device_ids=true, to_apply=%region_23.24 | all-reduce | flops 13314 | bytes 106512 | tf_op jit(solution)/shard_map/psum | solution.py:254
  695.1 20.0 %fusion.31 = bf16[1,577,4096]{2,1,0:T(8,128)(2,1)} fusion(bf16[577,2048]{1,0:T(8,128)(2,1)} %get-tuple-element.131, bf16[2048,4096]{1,0:T(8,128)(2,1)} %all-gather.22.cloned.1.call-done.rows_ref, f32[577,4096]{1,0:T(8,128)} %fusion.142, f32[577,4096]{1,0:T(8,128)} %fusion.141, f32[4096]{0:T(1024)S(1)} %copy-done.55), kind=kOutput, calls=%fused_computation.57 | convolution fusion | flops 9689907200 | bytes 42790912 | tf_op jit(solution)/shard_map/tc,cp->tp/dot_general | solution.py:26
  715.1 80.6 %shard_map.265 = bf16[8,5,584,1024]{3,2,1,0:T(8,128)(2,1)} custom-call(bf16[8,577,4096]{2,1,0:T(8,128)(2,1)} %copy.51.grad_ref, bf16[2048,4096]{1,0:T(8,128)(2,1)} %all-gather.22.cloned.1.call-done.rows_ref, bf16[8,5,584,1024]{3,2,1,0:T(8,128)(2,1)} %shard_map.264.rest_0_), custom_call_target="tpu_custom_call", output_to_operand_aliasing={{}: (2, {})} | custom-call | flops 68585259008 | bytes 71335936 | tf_op jit(solution)/shard_map/pallas_call | solution.py:85
  799.4 2.6 fusion.134
  802.0 8.6 %copy.89 = bf16[8,584,1024]{2,1,0:T(8,128)(2,1)} copy(bf16[8,584,1024]{2,1,0:T(8,128)(2,1)} %bitcast.289) | data formatting | bytes 19136512
  (201 shorter events, 46.6 us)
Async XLA Ops:
  7.2 77.0 %all-gather.14.cloned.1.call-start = ((), (), s32[]{:S(2)}) async-start(), calls=%async_computation.4 | async-start | bytes 9437184 | tf_op jit(solution)/shard_map/all_gather | solution.py:144
  9.6 154.8 %all-gather.16.cloned.1.call-start = ((), (), s32[]{:S(2)}) async-start(), calls=%async_computation.5 | async-start | bytes 9437184 | tf_op jit(solution)/shard_map/all_gather | solution.py:145
  10.4 185.4 %all-gather.18.cloned.1.call-start = ((), (), s32[]{:S(2)}) async-start(), calls=%async_computation.6 | async-start | bytes 9437184 | tf_op jit(solution)/shard_map/all_gather | solution.py:147
  11.2 225.3 %all-gather.12.cloned.1.call-start = ((), (), s32[]{:S(2)}) async-start(), calls=%async_computation.3 | async-start | bytes 18874368 | tf_op jit(solution)/shard_map/all_gather | solution.py:148
  48.6 8.7 %copy-start.29 = (f32[584]{0:T(1024)}, f32[584]{0:T(1024)S(1)}, u32[]{:S(2)}) copy-start(f32[584]{0:T(1024)S(1)} %fusion.118) | copy-start | bytes 7012
  48.6 115.8 %copy-start.27 = (f32[1,1024]{1,0:T(1,128)}, f32[1,1024]{1,0:T(1,128)S(1)}, u32[]{:S(2)}) copy-start(f32[1,1024]{1,0:T(1,128)S(1)} %get-tuple-element.166) | copy-start | bytes 12292
  48.6 115.8 %copy-start.49 = (f32[1,1024]{1,0:T(1,128)}, f32[1,1024]{1,0:T(1,128)S(1)}, u32[]{:S(2)}) copy-start(f32[1,1024]{1,0:T(1,128)S(1)} %get-tuple-element.169) | copy-start | bytes 12292
  51.0 36.8 %copy-start.16 = (bf16[584,1024]{1,0:T(8,128)(2,1)}, bf16[584,1024]{1,0:T(8,128)(2,1)S(1)}, u32[]{:S(2)}) copy-start(bf16[584,1024]{1,0:T(8,128)(2,1)S(1)} %fusion.53) | copy-start | bytes 3588100
  51.0 6.4 copy-start.52
  51.0 8.3 %copy-start.51 = (f32[512]{0:T(512)S(1)}, f32[512]{0:T(512)}, u32[]{:S(2)}) copy-start(f32[512]{0:T(512)} %param.25) | copy-start | bytes 6148
  57.3 254.7 %all-gather.24.cloned.1.call-start = ((), (), s32[]{:S(2)}) async-start(), calls=%async_computation.12 | async-start | bytes 10764288 | tf_op jit(solution)/shard_map/all_gather | solution.py:182
  84.2 80.3 %copy-start.44 = (f32[8,1,512]{2,1,0:T(1,128)}, f32[8,1,512]{2,1,0:T(1,128)S(1)}, u32[]{:S(2)}) copy-start(f32[8,1,512]{2,1,0:T(1,128)S(1)} %all-gather.2) | copy-start | bytes 49156
  84.2 31.9 %copy-start.53 = (pred[584]{0:T(1024)(128)(4,1)}, pred[584]{0:T(1024)(128)(4,1)S(1)}, u32[]{:S(2)}) copy-start(pred[584]{0:T(1024)(128)(4,1)S(1)} %iota_compare_fusion) | copy-start | bytes 1756
  144.1 9.5 %copy-start.1 = (bf16[584,3072]{0,1:T(8,128)(2,1)S(1)}, bf16[584,3072]{0,1:T(8,128)(2,1)}, u32[]{:S(2)}) copy-start(bf16[584,3072]{0,1:T(8,128)(2,1)} %copy.52) | copy-start | bytes 10764292
  163.3 32.5 %copy-start.3 = (bf16[584,1024]{1,0:T(8,128)(2,1)}, bf16[584,1024]{1,0:T(8,128)(2,1)S(1)}, u32[]{:S(2)}) copy-start(bf16[584,1024]{1,0:T(8,128)(2,1)S(1)} %get-tuple-element.121) | copy-start | bytes 3588100
  163.3 32.5 %copy-start.23 = (f32[584]{0:T(1024)}, f32[584]{0:T(1024)S(1)}, u32[]{:S(2)}) copy-start(f32[584]{0:T(1024)S(1)} %broadcast_multiply_fusion) | copy-start | bytes 7012
  164.4 31.4 %copy-start.37 = (f32[584]{0:T(1024)}, f32[584]{0:T(1024)S(1)}, u32[]{:S(2)}) copy-start(f32[584]{0:T(1024)S(1)} %fusion.119) | copy-start | bytes 7012
  164.5 31.4 %copy-start.47 = (f32[1024]{0:T(1024)S(1)}, f32[1024]{0:T(1024)}, u32[]{:S(2)}) copy-start(f32[1024]{0:T(1024)} %param.27) | copy-start | bytes 12292
  206.2 165.6 %all-gather.20.cloned.1.call-start = ((), (), s32[]{:S(2)}) async-start(), calls=%async_computation.7 | async-start | bytes 18874368 | tf_op jit(solution)/shard_map/all_gather | solution.py:148
  206.9 248.8 %all-gather.22.cloned.1.call-start = ((), (), s32[]{:S(2)}) async-start(), calls=%async_computation.8 | async-start | bytes 18874368 | tf_op jit(solution)/shard_map/all_gather | solution.py:148
  236.6 391.4 %reduce-scatter.4.cloned.1.call-start = ((), (), s32[]{:S(2)}) async-start(), calls=%async_computation.9 | async-start | bytes 9437184 | tf_op jit(solution)/shard_map/reduce_scatter | solution.py:221
  467.7 11.8 %copy-start.18 = (bf16[577,1024]{1,0:T(8,128)(2,1)}, bf16[577,1024]{1,0:T(8,128)(2,1)S(1)}, u32[]{:S(2)}) copy-start(bf16[577,1024]{1,0:T(8,128)(2,1)S(1)} %fusion.76) | copy-start | bytes 3545092
  467.7 11.8 %copy-start.45 = (f32[8,1,512]{2,1,0:T(1,128)S(1)}, f32[8,1,512]{2,1,0:T(1,128)}, u32[]{:S(2)}) copy-start(f32[8,1,512]{2,1,0:T(1,128)} %copy-done.44) | copy-start | bytes 49156
  479.5 17.2 %copy-start.4 = (bf16[584,1024]{1,0:T(8,128)(2,1)S(1)}, bf16[584,1024]{1,0:T(8,128)(2,1)}, u32[]{:S(2)}) copy-start(bf16[584,1024]{1,0:T(8,128)(2,1)} %copy-done.3) | copy-start | bytes 3588100
  479.5 17.2 %copy-start.24 = (f32[584]{0:T(1024)S(1)}, f32[584]{0:T(1024)}, u32[]{:S(2)}) copy-start(f32[584]{0:T(1024)} %copy-done.23) | copy-start | bytes 7012
  479.5 17.2 %copy-start.28 = (f32[1,1024]{1,0:T(1,128)S(1)}, f32[1,1024]{1,0:T(1,128)}, u32[]{:S(2)}) copy-start(f32[1,1024]{1,0:T(1,128)} %copy-done.27) | copy-start | bytes 12292
  479.5 17.2 %copy-start.38 = (f32[584]{0:T(1024)S(1)}, f32[584]{0:T(1024)}, u32[]{:S(2)}) copy-start(f32[584]{0:T(1024)} %copy-done.37) | copy-start | bytes 7012
  479.5 17.2 %copy-start.50 = (f32[1,1024]{1,0:T(1,128)S(1)}, f32[1,1024]{1,0:T(1,128)}, u32[]{:S(2)}) copy-start(f32[1,1024]{1,0:T(1,128)} %copy-done.49) | copy-start | bytes 12292
  518.0 110.1 %reduce-scatter.6.cloned.1.call-start = ((), (), s32[]{:S(2)}) async-start(), calls=%async_computation.10 | async-start | bytes 9437184 | tf_op jit(solution)/shard_map/reduce_scatter | solution.py:220
  518.8 280.6 %reduce-scatter.8.cloned.1.call-start = ((), (), s32[]{:S(2)}) async-start(), calls=%async_computation.11 | async-start | bytes 9437184 | tf_op jit(solution)/shard_map/reduce_scatter | solution.py:232
  544.0 8.0 copy-start.54
  602.1 13.3 %slice-start = ((s8[6291456]{0:T(1024)(128)(4,1)}), s8[2097152]{0:T(1024)(128)(4,1)S(1)}, s32[]{:S(2)}) async-start(s8[6291456]{0:T(1024)(128)(4,1)} %bitcast.291), calls=%async_computation.14 | async-start | bytes 4194304
  602.2 199.8 %all-gather.26.cloned.1.call-start = ((), (), s32[]{:S(2)}) async-start(), calls=%async_computation.13 | async-start | bytes 10764288 | tf_op jit(solution)/shard_map/all_gather | solution.py:240
  606.0 9.4 %slice-start.1 = ((s8[6291456]{0:T(1024)(128)(4,1)}), s8[4194304]{0:T(1024)(128)(4,1)S(1)}, s32[]{:S(2)}) async-start(s8[6291456]{0:T(1024)(128)(4,1)} %bitcast.291), calls=%async_computation.15 | async-start | bytes 8388608
  609.8 5.6 copy-start.11
  609.8 5.6 copy-start.26
  609.8 5.6 copy-start.32
  615.4 6.5 copy-start.33
  615.4 6.5 copy-start.40
  615.4 6.5 copy-start.30
  628.1 23.4 %slice-start.2 = ((s8[16777216]{0:T(1024)(128)(4,1)}), s8[4194304]{0:T(1024)(128)(4,1)S(1)}, s32[]{:S(2)}) async-start(s8[16777216]{0:T(1024)(128)(4,1)} %bitcast.301), calls=%async_computation.16 | async-start | bytes 8388608
  634.7 16.8 %slice-start.3 = ((s8[16777216]{0:T(1024)(128)(4,1)}), s8[4194304]{0:T(1024)(128)(4,1)S(1)}, s32[]{:S(2)}) async-start(s8[16777216]{0:T(1024)(128)(4,1)} %bitcast.301), calls=%async_computation.17 | async-start | bytes 8388608
  634.7 16.8 %slice-start.4 = ((s8[16777216]{0:T(1024)(128)(4,1)}), s8[4194304]{0:T(1024)(128)(4,1)S(1)}, s32[]{:S(2)}) async-start(s8[16777216]{0:T(1024)(128)(4,1)} %bitcast.301), calls=%async_computation.18 | async-start | bytes 8388608
  634.7 16.8 %slice-start.5 = ((s8[16777216]{0:T(1024)(128)(4,1)}), s8[4194304]{0:T(1024)(128)(4,1)S(1)}, s32[]{:S(2)}) async-start(s8[16777216]{0:T(1024)(128)(4,1)} %bitcast.301), calls=%async_computation.19 | async-start | bytes 8388608
  634.7 16.8 %copy-start.35 = (bf16[577,2048]{1,0:T(8,128)(2,1)S(1)}, bf16[577,2048]{1,0:T(8,128)(2,1)}, u32[]{:S(2)}) copy-start(bf16[577,2048]{1,0:T(8,128)(2,1)} %get-tuple-element.132) | copy-start | bytes 7090180
  651.5 13.8 %copy-start.43 = (f32[4096]{0:T(1024)S(1)}, f32[4096]{0:T(1024)}, u32[]{:S(2)}) copy-start(f32[4096]{0:T(1024)} %get-tuple-element.181) | copy-start | bytes 49156
  651.5 43.6 %copy-start.55 = (f32[4096]{0:T(1024)S(1)}, f32[4096]{0:T(1024)}, u32[]{:S(2)}) copy-start(f32[4096]{0:T(1024)} %param.29) | copy-start | bytes 49156
  715.1 80.6 %copy-start.19 = (bf16[512,1024]{1,0:T(8,128)(2,1)S(1)}, bf16[512,1024]{1,0:T(8,128)(2,1)}, u32[]{:S(2)}) copy-start(bf16[512,1024]{1,0:T(8,128)(2,1)} %reduce-scatter.4.cloned.1.call-done) | copy-start | bytes 3145732
  (27 other events, 59.1 us)
Sparse Core Ops, SparseCore 0:
  10.2 48.2 all-gather.13
  60.1 45.7 all-gather.15
  107.5 45.6 all-gather.17
  155.2 81.2 all-gather.11
  238.0 50.9 all-gather.23
  290.5 81.3 all-gather.19
  374.0 81.6 all-gather.21
  518.1 48.9 reduce-scatter.3
  569.4 48.0 reduce-scatter.5
  619.6 48.0 reduce-scatter.7
  669.3 50.4 all-gather.25

commit v2 on v1

--- a/solution.py
+++ b/solution.py
@@ -30,13 +30,80 @@
     return lax.optimization_barrier((value, earlier))
 
 
-def attend(real_rows, q_act, k_act, v_act):
-    tokens = q_act.shape[0]
-    score_scale = q_act.shape[2] ** -0.5
-    scores = matmul('qhe,khe->hqk', q_act, k_act) * score_scale
-    key_ok = (jnp.arange(tokens) < real_rows)[None, None, :]
-    attn_probs = jax.nn.softmax(jnp.where(key_ok, scores, -1e30), axis=-1).astype(jnp.bfloat16)
-    return matmul('hqk,khe->qhe', attn_probs, v_act).astype(jnp.bfloat16)
+def head_probs(real_rows, q_act, k_pad):
+    scores = lax.dot_general(q_act, k_pad, (((1,), (1,)), ((), ())), preferred_element_type=jnp.float32)
+    key_ok = lax.broadcasted_iota(jnp.int32, scores.shape, 1) < real_rows
+    scores = jnp.where(key_ok, scores * q_act.shape[1] ** -0.5, -1e30)
+    raised = jnp.exp(scores - jnp.max(scores, axis=-1, keepdims=True))
+    return raised / jnp.sum(raised, axis=-1, keepdims=True)
+
+
+def pad_keys(pads, refs):
+    tokens = refs[0].shape[0]
+    for pad_ref, ref in zip(pads, refs):
+        pad_ref[0:tokens, :] = ref[...]
+        pad_ref[tokens:, :] = jnp.zeros((pad_ref.shape[0] - tokens, pad_ref.shape[1]), pad_ref.dtype)
+
+
+def attend_kernel(real_rows, head_dim, q_ref, k_ref, v_ref, out_ref, k_pad, v_pad):
+    pad_keys((k_pad, v_pad), (k_ref, v_ref))
+    for at in range(0, q_ref.shape[1], head_dim):
+        cols = slice(at, at + head_dim)
+        probs = head_probs(real_rows, q_ref[:, cols], k_pad[:, cols]).astype(jnp.bfloat16)
+        out_ref[:, cols] = jnp.dot(probs, v_pad[:, cols], preferred_element_type=jnp.float32).astype(jnp.bfloat16)
+
+
+def attend_grad_kernel(real_rows, head_dim, q_ref, k_ref, v_ref, grad_ref, out_ref, k_pad, v_pad):
+    pad_keys((k_pad, v_pad), (k_ref, v_ref))
+    tokens = q_ref.shape[0]
+    over_rows = (((0,), (0,)), ((), ()))
+    for at in range(0, q_ref.shape[1], head_dim):
+        cols = slice(at, at + head_dim)
+        q_act, grad = q_ref[:, cols], grad_ref[:, cols]
+        probs = head_probs(real_rows, q_act, k_pad[:, cols])
+        grad_v = lax.dot_general(probs.astype(jnp.bfloat16), grad, over_rows, preferred_element_type=jnp.float32)
+        grad_p = lax.dot_general(grad, v_pad[:, cols], (((1,), (1,)), ((), ())), preferred_element_type=jnp.float32)
+        grad_p = grad_p.astype(jnp.bfloat16).astype(jnp.float32)
+        centre = jnp.sum(probs * grad_p, axis=-1, keepdims=True)
+        grad_s = (probs * (grad_p - centre) * head_dim ** -0.5).astype(jnp.bfloat16)
+        grad_k = lax.dot_general(grad_s, q_act, over_rows, preferred_element_type=jnp.float32)
+        grad_q = jnp.dot(grad_s, k_pad[:, cols], preferred_element_type=jnp.float32)
+        out_ref[0, :, cols] = grad_q.astype(jnp.bfloat16)
+        out_ref[1, :, cols] = grad_k[0:tokens].astype(jnp.bfloat16)
+        out_ref[2, :, cols] = grad_v[0:tokens].astype(jnp.bfloat16)
+
+
+def attend(real_rows, head_dim, width, qkv, grad=None):
+    tokens = qkv.shape[0]
+    lanes = max(128, head_dim)
+    steps = width // lanes
+    keys = (tokens + 127) // 128 * 128
+    part = lambda n: pl.BlockSpec((tokens, lanes), lambda h, n=n: (0, n * steps + h))
+    one = 2 * tokens * keys * width
+    args, in_specs = [qkv, qkv, qkv], [part(0), part(1), part(2)]
+    if grad is None:
+        kernel, dots = attend_kernel, 2
+        out_shape, out_specs = (tokens, width), part(0)
+    else:
+        kernel, dots = attend_grad_kernel, 5
+        args, in_specs = args + [grad], in_specs + [part(0)]
+        out_shape, out_specs = (3, tokens, width), pl.BlockSpec((3, tokens, lanes), lambda h: (0, 0, h))
+    return pl.pallas_call(
+        functools.partial(kernel, real_rows, head_dim),
+        grid=(steps,),
+        out_shape=jax.ShapeDtypeStruct(out_shape, jnp.bfloat16),
+        in_specs=in_specs,
+        out_specs=out_specs,
+        scratch_shapes=[pltpu.VMEM((keys, lanes), jnp.bfloat16)] * 2,
+        compiler_params=pltpu.CompilerParams(dimension_semantics=("arbitrary",), vmem_limit_bytes=40 * 1024 * 1024),
+        cost_estimate=pl.CostEstimate(flops=4 * dots * one, bytes_accessed=16 * tokens * width, transcendentals=0),
+    )(*args)
+
+
+def split_exact(values):
+    high = lax.reduce_precision(values, 8, 7)
+    mid = lax.reduce_precision(values - high, 8, 7)
+    return jnp.stack([high, mid, values - high - mid]).astype(jnp.bfloat16)
 
 
 def feats_kernel(blocks, piece, real_rows, grad_ref, rows_ref, *rest):
@@ -131,20 +198,20 @@
     tile_count, tokens, width = hidden.shape
     real_rows = proj_grad.shape[1]
     feats = inter_feats.shape[2]
-    feat_local, proj_dim = w_proj.shape
+    feat_local, _ = w_proj.shape
     local_heads, head_dim = w_query.shape[1:]
     local_width = local_heads * head_dim
     group = lax.axis_size('tp')
-    heads = group * local_heads
     mine = lax.axis_index('tp')
     piece = math.gcd(feat_local, width)
     per_dev, per_feat = feat_local // piece, width // piece
 
     flip = lambda w: w.reshape(width, local_width).T
     w_attn = lax.all_gather(jnp.stack([flip(w_query), flip(w_key), flip(w_value), w_out.reshape(local_width, width)]), 'tp', axis=1, tiled=True)
-    fc1 = lax.all_gather(w_fc1, 'tp', axis=1, tiled=True)
+    w_mlp = lax.all_gather(jnp.stack([w_fc1.T, w_fc2]), 'tp', axis=1, tiled=True)
+    fc1, fc2 = w_mlp[0], w_mlp[1]
     bias1 = lax.all_gather(b_fc1, 'tp', axis=0, tiled=True)
-    fc2 = lax.all_gather(w_fc2, 'tp', axis=0, tiled=True)
+    proj_grad, bias1 = after(proj_grad, bias1)
     gather_rows = lambda part: lax.all_gather(part, 'tp', axis=0, tiled=True)
     w_parts = [w_proj[j * piece:(j + 1) * piece] for j in range(per_dev)]
 
@@ -153,16 +220,14 @@
     proj_grad = with_layout_constraint(proj_grad, Layout((0, 1, 2)))
     normed, (proj_grad, w_parts[0]) = after(normed, (proj_grad, w_parts[0]))
     proj_rows = [gather_rows(w_parts[0])]
-    w_qkv = w_attn[:3].reshape(3 * width, width)
-    qkv = matmul('td,jd->tj', normed, w_qkv).astype(jnp.bfloat16).reshape(tokens, 3, heads, head_dim)
-    context, attend_pull = jax.vjp(functools.partial(attend, real_rows), qkv[:, 0], qkv[:, 1], qkv[:, 2])
-    context = context.reshape(tokens, width)
+    qkv = matmul('td,jd->tj', normed, w_attn.reshape(-1, width)).astype(jnp.bfloat16)
+    context = attend(real_rows, head_dim, width, qkv)
     attn_out = matmul('tj,jd->td', context, w_attn[3])
     gate_attn = jnp.tanh(gate_params[0])
     gate_mlp = jnp.tanh(gate_params[1])
     x_one_wide = (x_wide + gate_attn * attn_out).astype(jnp.bfloat16).astype(jnp.float32)
     normed_two, norm2_pull = jax.vjp(layer_norm, x_one_wide, ln_params[2], ln_params[3])
-    pre_act = matmul('td,df->tf', normed_two, fc1) + bias1
+    pre_act = matmul('td,fd->tf', normed_two, fc1) + bias1
     mlp_act, gelu_pull = jax.vjp(gelu_bf16, pre_act)
     mlp_out = matmul('tf,fd->td', mlp_act, fc2) + b_fc2
     x_two = (x_one_wide + gate_mlp * mlp_out).astype(jnp.bfloat16)
@@ -178,28 +243,18 @@
                 blocks.append((d, at // per_feat - 1, at % per_feat))
         return grad_feats_part(proj_grad, proj_rows[j], tuple(blocks), piece, feats, tokens, width, prior)
 
-    w_parts[1], x_two = after(w_parts[1], x_two)
-    x_two_all = lax.all_gather(x_two, 'tp', axis=0, tiled=False)
+    w_parts[1], w_attn = after(w_parts[1], w_attn)
     proj_rows.append(gather_rows(w_parts[1]))
     proj_rows[0], x_two = after(proj_rows[0], x_two)
     for part in w_parts[2:]:
         part, proj_rows[0] = after(part, proj_rows[0])
         proj_rows.append(gather_rows(part))
     grad_inter = feats_part(0, None)
-    x_two_all, grad_inter = after(x_two_all, grad_inter)
-
-    cols = []
-    for j in range(per_dev):
-        at = mine * per_dev + j
-        feat, col = at // per_feat, (at % per_feat) * piece
-        from_two = lax.dynamic_slice_in_dim(x_two_all, col, piece, axis=2)
-        from_inter = lax.dynamic_slice(inter, (0, jnp.maximum(feat - 1, 0), 0, col), (tile_count, 1, tokens, piece))[:, 0]
-        cols.append(jnp.where(feat == 0, from_two, from_inter))
-    feats_local = jnp.concatenate(cols, axis=-1)
-    grad_w_proj = rows_grad(feats_local, proj_grad)
     for j in range(1, per_dev - 1):
-        proj_rows[j], grad_w_proj = after(proj_rows[j], grad_w_proj)
+        proj_rows[j], grad_inter = after(proj_rows[j], grad_inter)
         grad_inter = feats_part(j, grad_inter)
+    x_two, proj_rows[-2] = after(x_two, proj_rows[-2])
+    x_two_all = lax.all_gather(x_two, 'tp', axis=0, tiled=False)
     proj_rows[-1], grad_inter = after(proj_rows[-1], grad_inter)
 
     rows_two = jnp.concatenate([proj_rows[at % per_dev][(at // per_dev) * piece:(at // per_dev + 1) * piece] for at in range(per_feat)], axis=0)
@@ -215,7 +270,7 @@
     grad_b_fc1 = jnp.sum(grad_pre, axis=0)
     grad_pre_low = grad_pre.astype(jnp.bfloat16)
     grad_fc1 = matmul('tf,td->fd', grad_pre_low, normed_two).astype(jnp.bfloat16)
-    grad_normed_two = matmul('tf,df->td', grad_pre_low, fc1).astype(jnp.bfloat16)
+    grad_normed_two = matmul('tf,fd->td', grad_pre_low, fc1).astype(jnp.bfloat16)
     grad_normed_two, (grad_fc1, grad_fc2) = after(grad_normed_two, (grad_fc1, grad_fc2))
     grad_w_fc2 = lax.psum_scatter(grad_fc2, 'tp', scatter_dimension=0, tiled=True)
     grad_w_fc1 = lax.psum_scatter(grad_fc1, 'tp', scatter_dimension=0, tiled=True)
@@ -225,20 +280,45 @@
     grad_gate_attn = jnp.sum(grad_x_one * attn_out) * (1.0 - gate_attn * gate_attn)
     grad_attn_low = grad_attn.astype(jnp.bfloat16)
     grad_wo = matmul('tj,td->jd', context, grad_attn_low)
-    grad_context = matmul('td,jd->tj', grad_attn_low, w_attn[3]).astype(jnp.bfloat16).reshape(tokens, heads, head_dim)
-    grad_qkv = jnp.stack(attend_pull(grad_context), axis=1).reshape(tokens, 3 * width)
-    grad_wqkv = matmul('tj,td->jd', grad_qkv, normed).reshape(3, width, width)
+    grad_context = matmul('td,jd->tj', grad_attn_low, w_attn[3]).astype(jnp.bfloat16)
+    grad_qkv = attend(real_rows, head_dim, width, qkv, grad_context)
+    grad_wqkv = matmul('gtj,td->gjd', grad_qkv, normed)
     grad_w_attn = jnp.concatenate([grad_wqkv, grad_wo[None]]).astype(jnp.bfloat16)
     grad_w_attn = lax.psum_scatter(grad_w_attn, 'tp', scatter_dimension=1, tiled=True).astype(jnp.float32)
     unflip = lambda g: g.T.reshape(width, local_heads, head_dim)
-    grad_normed = matmul('tj,jd->td', grad_qkv, w_qkv).astype(jnp.bfloat16)
+    grad_normed = matmul('gtj,gjd->td', grad_qkv, w_attn[:3]).astype(jnp.bfloat16)
     grad_x_ln, grad_gain, grad_bias = norm1_pull(grad_normed)
     grad_tile = (grad_x_one + grad_x_ln).astype(jnp.bfloat16)
 
+    x_two_all, grad_tile = after(x_two_all, grad_tile)
+    cols = []
+    for j in range(per_dev):
+        at = mine * per_dev + j
+        feat, col = at // per_feat, (at % per_feat) * piece
+        from_two = lax.dynamic_slice_in_dim(x_two_all, col, piece, axis=2)
+        from_inter = lax.dynamic_slice(inter, (0, jnp.maximum(feat - 1, 0), 0, col), (tile_count, 1, tokens, piece))[:, 0]
+        cols.append(jnp.where(feat == 0, from_two, from_inter))
+    grad_w_proj = rows_grad(jnp.concatenate(cols, axis=-1), proj_grad)
+
+    grad_b_proj = jnp.sum(grad_mine, axis=0, dtype=jnp.float32)
+    small = [grad_gain, grad_bias, grad_gain_two, grad_bias_two, grad_b_fc2, grad_b_fc1, grad_b_proj, jnp.stack([grad_gate_attn, grad_gate_mlp])]
+    lines = [-(-v.shape[0] // width) for v in small]
+    ends = [sum(lines[:n + 1]) for n in range(len(small))]
+    total = -(-ends[-1] // 8) * 8
+    small = jnp.concatenate([jnp.pad(v, (0, n * width - v.shape[0])).reshape(n, width) for v, n in zip(small, lines)])
+    terms = split_exact(jnp.pad(small, ((0, total - ends[-1]), (0, 0)))).reshape(3 * total, width)
+    grad_tile, (grad_w_fc1, grad_w_fc2) = after(grad_tile, (grad_w_fc1, grad_w_fc2))
+    grad_tile, grad_w_proj = after(grad_tile, grad_w_proj)
+    gathered = lax.all_gather(jnp.concatenate([grad_tile, terms]), 'tp', axis=0, tiled=False)
+    grad_hidden = gathered[:, :tokens]
+    sums = jnp.sum(gathered[:, tokens:].reshape(group * 3, total, width).astype(jnp.float32), axis=0)
+    grad_ln, grad_b_fc2 = sums[:4], sums[4]
+    grad_b_fc1 = lax.dynamic_slice_in_dim(sums[ends[4]:ends[5]].reshape(-1), mine * b_fc1.shape[0], b_fc1.shape[0], axis=0)
+    grad_b_proj = sums[ends[5]:ends[6]].reshape(-1)[:b_proj.shape[0]]
+    grad_gates = sums[ends[6], :2]
+    grad_w_fc1, grad_w_fc2 = grad_w_fc1.astype(jnp.float32).T, grad_w_fc2.astype(jnp.float32)
+
     proj_rows[-1], grad_tile = after(proj_rows[-1], grad_tile)
-    grad_tile, (grad_w_fc1, grad_w_fc2) = after(grad_tile, (grad_w_fc1, grad_w_fc2))
-    grad_hidden = lax.all_gather(grad_tile, 'tp', axis=0, tiled=False)
-    grad_w_fc1, grad_w_fc2 = grad_w_fc1.astype(jnp.float32).T, grad_w_fc2.astype(jnp.float32)
     grad_inter = jnp.transpose(feats_part(per_dev - 1, grad_inter), (0, 2, 1, 3))
     inter_mine = lax.dynamic_index_in_dim(inter, mine, 0, keepdims=False)
     feats_mine = jnp.concatenate([x_two[None], inter_mine], axis=0)[:, :real_rows]
@@ -248,14 +328,6 @@
                                 for at in range(j, group * per_dev, per_dev)], axis=-1)
         proj_sum = proj_sum + matmul('tc,cp->tp', part, proj_rows[j])
     proj_out = proj_sum.astype(jnp.bfloat16)[None]
-
-    grad_b_proj = jnp.sum(grad_mine, axis=0, dtype=jnp.float32)
-    small = [grad_gain, grad_bias, grad_gain_two, grad_bias_two, grad_b_fc2, grad_b_fc1, grad_b_proj, jnp.stack([grad_gate_attn, grad_gate_mlp])]
-    sums = lax.psum(jnp.concatenate(small), 'tp')
-    ends = [sum(s.shape[0] for s in small[:n + 1]) for n in range(len(small))]
-    grad_gain, grad_bias, grad_gain_two, grad_bias_two, grad_b_fc2, grad_b_fc1, grad_b_proj, grad_gates = jnp.split(sums, ends[:-1])
-    grad_ln = jnp.stack([grad_gain, grad_bias, grad_gain_two, grad_bias_two])
-    grad_b_fc1 = lax.dynamic_slice_in_dim(grad_b_fc1, mine * b_fc1.shape[0], b_fc1.shape[0], axis=0)
     return (proj_out, grad_hidden, grad_inter, unflip(grad_w_attn[0]), unflip(grad_w_attn[1]), unflip(grad_w_attn[2]), grad_w_attn[3].reshape(local_heads, head_dim, width), grad_ln, grad_gates, grad_w_fc1, grad_b_fc1, grad_w_fc2, grad_b_fc2, grad_w_proj, grad_b_proj)
 
 
@@ -266,4 +338,5 @@
     in_specs = (tiles_spec, inter_spec, tiles_spec, head_cols, head_cols, head_cols, P('tp', None, None), P(None, None), P(None), P(None, 'tp'), P('tp'), P('tp', None), P(None), P('tp', None), P(None))
     grad_heads = P('dp', 'tp', None)
     out_specs = (P(('dp', 'tp'), None, None), tiles_spec, inter_spec, grad_heads, grad_heads, grad_heads, P(('dp', 'tp'), None, None), P('dp', None), P('dp'), P('dp', 'tp'), P(('dp', 'tp')), P(('dp', 'tp'), None), P('dp'), P(('dp', 'tp'), None), P('dp'))
+
     return jax.shard_map(local_step, mesh=mesh, in_specs=in_specs, out_specs=out_specs, check_vma=False)

time: 822 us -> 773 us (0.940)
  Pallas kernels: 281 us -> 341 us
  matrix products: 234 us -> 178 us
  other arithmetic: 98.4 us -> 45.2 us
  waiting for transfers between devices: 36.2 us -> 78 us
  blocking collectives: 51.6 us -> 24.8 us
  local copies, waits for them, and re-layouts: 96.9 us -> 77.7 us
    dot_general x22 -> x16, matrix products: 234 us -> 178 us  [matmul(): jnp.einsum(eq_form, lhs_in, rhs_in, preferred_element_type=jnp.float32)]
    pallas_call x0 -> x2, Pallas kernels: none -> 56.3 us  [attend(): pl.pallas_call(functools.partial(kernel, real_rows, head_dim), grid=(step...]
    unnamed x135 -> x127, local copies, waits for them, and re-layouts: 62.7 us -> 10.6 us
    optimization_barrier x0 -> x1, local copies, waits for them, and re-layouts: none -> 33.9 us  [after(): return lax.optimization_barrier((value, earlier))]
    sub x1 -> x0, other arithmetic: 27.3 us -> none  [attend(): jax.nn.softmax(jnp.where(key_ok, scores, -1e+30), axis=-1)]
    psum x1 -> x0, blocking collectives: 26.8 us -> none  [local_step(): sums = lax.psum(jnp.concatenate(small), 'tp')]
    all_gather x3, waiting for transfers between devices: 33.1 us -> 55.2 us  [local_step(): gather_rows = lambda part: lax.all_gather(part, 'tp', axis=0, tiled=True)]
    all_gather x3 -> x2, waiting for transfers between devices: 0.02 us -> 21.1 us  [the longest x1 21 us: local_step(): lax.all_gather(jnp.stack([w_fc1.T, w_fc2]), 'tp', axis=1, tiled=True)]
  transfers between devices with their start and end apart: 11 -> 10, of which waited for: 3 -> 3; matrix products, arithmetic and copies ran while one was open for 42% -> 36% of each run, Pallas kernels for 34% -> 45%
where the time goes in v2:
time: 773 us; the launch traced here: 764 us
  Pallas kernels  341 us (44%)
  matrix products  178 us (23%)
  waiting for transfers between devices  78 us (10%)
  local copies, waits for them, and re-layouts  77.7 us (10%)
  other arithmetic  45.2 us (6%)
  blocking collectives  24.8 us (3%)
  between operations  18.3 us (2%)
    pallas_call x3, Pallas kernels, grad_feats_part(): pl.pallas_call(functools.partial(feats_kernel, blocks, piece, real_rows),...  236 us
    dot_general x16, matrix products, matmul(): jnp.einsum(eq_form, lhs_in, rhs_in, preferred_element_type=jnp.float32)  178 us
    pallas_call x2, Pallas kernels, attend(): pl.pallas_call(functools.partial(kernel, real_rows, head_dim), grid=(step...  56.3 us
    all_gather x3, waiting for transfers between devices, local_step(): gather_rows = lambda part: lax.all_gather(part, 'tp', axis=0, tiled=True)  55.2 us
    pallas_call x1, Pallas kernels, rows_grad(): pl.pallas_call(functools.partial(rows_grad_kernel, real_rows, min(512, de...  49.1 us
    optimization_barrier x1, local copies, waits for them, and re-layouts, after(): return lax.optimization_barrier((value, earlier))  33.9 us
    all_gather x1, blocking collectives, local_step(): bias1 = lax.all_gather(b_fc1, 'tp', axis=0, tiled=True)  24.8 us
    all_gather x1, waiting for transfers between devices, local_step(): lax.all_gather(jnp.stack([w_fc1.T, w_fc2]), 'tp', axis=1, tiled=True)  21 us
  transfers between devices with their start and end apart: 10, of which 3 were waited for; matrix products, arithmetic and copies ran while one was open for 36% of the time, Pallas kernels for 45%

profile of v2, /device:TPU:112, one launch (start us, length us, event | category | flops | bytes accessed | tf_op | source)
XLA Modules:
  0.0 763.9 jit_solution(16463226904007540920)
XLA Ops:
  7.3 2.4 pad_maximum_fusion.4
  12.1 24.8 %all-gather.2 = f32[8,1,512]{2,1,0:T(1,128)S(1)} all-gather(f32[1,1,512]{2,1,0:T(1,128)S(1)} %bitcast.325), channel_id=1, replica_groups=mesh['dp'=2,'tp'=8] {'tp'}, dimensions={0}, use_global_device_ids=true | all-gather | bytes 18432 | tf_op jit(solution)/shard_map/all_gather | solution.py:213
  36.9 33.9 %copy.35.grad_ref = bf16[8,577,4096]{2,1,0:T(8,128)(2,1)} copy(bf16[8,577,4096]{2,0,1:T(8,128)(2,1)} %param.17) | data formatting | bytes 75628544 | tf_op jit(solution)/shard_map/optimization_barrier | solution.py:30
  70.8 1.6 convert_reduce_fusion.4
  72.4 1.7 fusion.50
  74.8 1.8 fusion.49
  76.6 6.4 fusion.131
  85.8 8.9 %convolution_convert_fusion.2.q_ref.k_ref.v_ref = bf16[584,4096]{1,0:T(8,128)(2,1)S(1)} fusion(bf16[584,1024]{1,0:T(8,128)(2,1)S(1)} %fusion.49, bf16[4096,1024]{1,0:T(8,128)(2,1)} %bitcast.326), kind=kOutput, calls=%fused_computation.47 | convolution fusion | flops 4901339136 | bytes 14368768 | tf_op jit(solution)/shard_map/td,jd->tj/dot_general | solution.py:26
  94.8 19.7 %shard_map.262 = bf16[584,1024]{1,0:T(8,128)(2,1)S(1)} custom-call(bf16[584,4096]{1,0:T(8,128)(2,1)S(1)} %convolution_convert_fusion.2.q_ref.k_ref.v_ref, bf16[584,4096]{1,0:T(8,128)(2,1)S(1)} %convolution_convert_fusion.2.q_ref.k_ref.v_ref, bf16[584,4096]{1,0:T(8,128)(2,1)S(1)} %convolution_convert_fusion.2.q_ref.k_ref.v_ref), custom_call_target="tpu_custom_call" | custom-call | flops 6123683840 | bytes 9568256 | tf_op jit(solution)/shard_map/pallas_call | solution.py:91
  114.5 5.3 convert_reduce_fusion.3
  120.9 21.0 %all-gather.15.cloned.1.call-done = bf16[2,4096,1024]{2,1,0:T(8,128)(2,1)} async-done(((bf16[2,512,1024]{2,1,0:T(8,128)(2,1)}), bf16[2,4096,1024]{2,1,0:T(8,128)(2,1)}) %all-gather.15.cloned.1.call-update) | async-done | bytes 16777232 | tf_op jit(solution)/shard_map/all_gather | solution.py:211
  141.9 30.4 %multiply_convert_fusion = (bf16[584,4096]{1,0:T(8,128)(2,1)S(1)}, f32[584,4096]{1,0:T(8,128)}, f32[584,4096]{1,0:T(8,128)}) fusion(f32[4096]{0:T(1024)S(1)} %bitcast.319, bf16[2,4096,1024]{2,1,0:T(8,128)(2,1)} %all-gather.15.cloned.1.call-done, bf16[584,1024]{1,0:T(8,128)(2,1)S(1)} %get-tuple-element.116, f32[1024]{0:T(1024)S(1)} %bitcast.323, ...), kind=kOutput, calls=%fused_computation.12 | convolution fusion | flops 5060411392 | bytes 33534528 | tf_op jit(solution)/shard_map/td,fd->tf/dot_general | solution.py:26
  172.4 2.1 copy-done.48
  174.5 7.1 fusion.55
  181.6 43.9 %all-gather.11.cloned.1.call-done.rows_ref = bf16[2048,4096]{1,0:T(8,128)(2,1)} async-done(((bf16[256,4096]{1,0:T(8,128)(2,1)}), bf16[2048,4096]{1,0:T(8,128)(2,1)}) %all-gather.11.cloned.1.call-update) | async-done | bytes 16777232 | tf_op jit(solution)/shard_map/all_gather | solution.py:215
  225.7 71.5 %shard_map.263.rest_0_ = bf16[8,5,584,1024]{3,2,1,0:T(8,128)(2,1)} custom-call(bf16[8,577,4096]{2,1,0:T(8,128)(2,1)} %copy.35.grad_ref, bf16[2048,4096]{1,0:T(8,128)(2,1)} %all-gather.11.cloned.1.call-done.rows_ref), custom_call_target="tpu_custom_call" | custom-call | flops 58787364864 | bytes 68943872 | tf_op jit(solution)/shard_map/pallas_call | solution.py:152
  297.2 11.3 %all-gather.17.cloned.1.call-done.rows_ref = bf16[2048,4096]{1,0:T(8,128)(2,1)} async-done(((bf16[256,4096]{1,0:T(8,128)(2,1)}), bf16[2048,4096]{1,0:T(8,128)(2,1)}) %all-gather.17.cloned.1.call-update) | async-done | bytes 16777232 | tf_op jit(solution)/shard_map/all_gather | solution.py:215
  308.6 4.8 fusion.130
  313.3 83.4 %shard_map.264.rest_0_ = bf16[8,5,584,1024]{3,2,1,0:T(8,128)(2,1)} custom-call(bf16[8,577,4096]{2,1,0:T(8,128)(2,1)} %copy.35.grad_ref, bf16[2048,4096]{1,0:T(8,128)(2,1)} %all-gather.17.cloned.1.call-done.rows_ref, bf16[8,5,584,1024]{3,2,1,0:T(8,128)(2,1)} %shard_map.263.rest_0_), custom_call_target="tpu_custom_call", output_to_operand_aliasing={{}: (2, {})} | custom-call | flops 68585259008 | bytes 71335936 | tf_op jit(solution)/shard_map/pallas_call | solution.py:152
  396.8 1.6 slice-done.2
  399.2 12.0 %fusion.77 = bf16[577,1024]{1,0:T(8,128)(2,1)S(1)} fusion(bf16[256,4096]{1,0:T(8,128)(2,1)} %get-tuple-element.121, bf16[256,4096]{1,0:T(8,128)(2,1)S(1)} %slice-done.3, bf16[256,4096]{1,0:T(8,128)(2,1)S(1)} %slice-done.2, bf16[256,4096]{1,0:T(8,128)(2,1)} %get-tuple-element.120, bf16[8,577,4096]{2,1,0:T(8,128)(2,1)} %copy.35.grad_ref, s32[]{:T(128)S(6)} %select_n.71), kind=kOutput, calls=%fused_computation.122 | convolution fusion | flops 4874372096 | bytes 14354436 | tf_op jit(solution)/shard_map/tp,cp->tc/dot_general | solution.py:26
  411.2 9.3 %convolution_convert_fusion = bf16[4096,1024]{1,0:T(8,128)(2,1)} fusion(bf16[584,4096]{1,0:T(8,128)(2,1)S(1)} %bitcast.329, f32[]{:T(128)} %bitcast.18, bf16[577,1024]{1,0:T(8,128)(2,1)S(1)} %fusion.77), kind=kOutput, calls=%fused_computation.37 | convolution fusion | flops 4904935424 | bytes 14354436 | tf_op jit(solution)/shard_map/tf,td->fd/dot_general | solution.py:26
  420.6 16.8 %fusion.135 = (f32[4096]{0:T(1024)S(1)}, bf16[584,4096]{1,0:T(8,128)(2,1)}) fusion(f32[584,4096]{1,0:T(8,128)} %get-tuple-element.114, bf16[2,4096,1024]{2,1,0:T(8,128)(2,1)} %all-gather.15.cloned.1.call-done, f32[]{:T(128)} %bitcast.18, bf16[577,1024]{1,0:T(8,128)(2,1)S(1)} %fusion.77, f32[584,4096]{1,0:T(8,128)} %get-tuple-element.167, ...), kind=kOutput, calls=%fused_computation.213 | convolution fusion | flops 4943794176 | bytes 33524224 | tf_op jit(solution)/shard_map/td,fd->tf/dot_general | solution.py:26
  437.4 9.2 %fusion.74 = bf16[584,1024]{1,0:T(8,128)(2,1)S(1)} fusion(bf16[2,4096,1024]{2,1,0:T(8,128)(2,1)} %all-gather.15.cloned.1.call-done, bf16[584,4096]{1,0:T(8,128)(2,1)} %get-tuple-element.172), kind=kOutput, calls=%fused_computation.121 | convolution fusion | flops 4899545088 | bytes 14368768 | tf_op jit(solution)/shard_map/tf,fd->td/dot_general | solution.py:26
  446.7 9.7 %convolution_convert_fusion.1 = bf16[4096,1024]{1,0:T(8,128)(2,1)} fusion(bf16[584,4096]{1,0:T(8,128)(2,1)S(1)} %copy-done.49, bf16[584,1024]{1,0:T(8,128)(2,1)S(1)} %copy-done.5, f32[1024]{0:T(1024)S(1)} %bitcast.324, f32[1024]{0:T(1024)S(1)} %bitcast.305, f32[584]{0:T(1024)S(1)} %copy-done.32, f32[584]{0:T(1024)S(1)} %copy-done.20), kind=kOutput, calls=%fused_computation.38 | convolution fusion | flops 4906729472 | bytes 14381632 | tf_op jit(solution)/shard_map/tf,td->fd/dot_general | solution.py:26
  459.7 4.6 fusion.57
  464.3 3.2 convert_bitcast_fusion.2
  467.5 3.1 fusion.71.grad_ref
  470.6 36.6 %shard_map.265 = bf16[3,584,1024]{2,1,0:T(8,128)(2,1)S(1)} custom-call(bf16[584,4096]{1,0:T(8,128)(2,1)S(1)} %bitcast.284, bf16[584,4096]{1,0:T(8,128)(2,1)S(1)} %bitcast.284, bf16[584,4096]{1,0:T(8,128)(2,1)S(1)} %bitcast.284, bf16[584,1024]{1,0:T(8,128)(2,1)S(1)} %fusion.71.grad_ref), custom_call_target="tpu_custom_call" | custom-call | flops 15309209600 | bytes 9568256 | tf_op jit(solution)/shard_map/pallas_call | solution.py:91
  507.3 1.8 copy-done.3
  509.1 5.5 convolution_convert_fusion.3
  514.6 5.6 pad_maximum_fusion
  520.6 3.5 convert_reduce_fusion
  525.6 8.5 %convert_reduce_fusion.1 = (f32[1024]{0:T(1024)S(1)}, f32[584]{0:T(1024)S(1)}, bf16[584,1024]{1,0:T(8,128)(2,1)S(1)}) fusion(f32[1024]{0:T(1024)S(1)} %bitcast.310, f32[584]{0:T(1024)S(1)} %copy-done.22, bf16[8,584,1024]{2,1,0:T(8,128)(2,1)} %param.15, s32[]{:T(128)S(6)} %select_n.71, bf16[3,584,1024]{2,1,0:T(8,128)(2,1)} %copy-done.3, ...), kind=kOutput, calls=%fused_computation.53 | convolution fusion | flops 3678992896 | bytes 12284484 | tf_op jit(solution)/shard_map/gtj,gjd->td/dot_general | solution.py:26
  534.1 2.8 fusion.62
  537.1 3.3 fusion.60
  540.4 7.1 bitcast_select_fusion.2
  547.5 3.3 pad_maximum_fusion.1.feats_ref
  550.8 49.1 %shard_map.266 = f32[768,4096]{1,0:T(8,128)} custom-call(bf16[8,584,768]{2,1,0:T(8,128)(2,1)} %pad_maximum_fusion.1.feats_ref, bf16[8,577,4096]{2,1,0:T(8,128)(2,1)} %copy.35.grad_ref), custom_call_target="tpu_custom_call" | custom-call | flops 29393682432 | bytes 57573376 | tf_op jit(solution)/shard_map/pallas_call | solution.py:185
  601.2 3.6 dynamic-slice_bitcast_fusion
  607.3 16.5 %fusion.137 = f32[577,4096]{1,0:T(8,128)} fusion(bf16[577,2048]{1,0:T(8,128)(2,1)S(1)} %get-tuple-element.127, bf16[2048,4096]{1,0:T(8,128)(2,1)} %all-gather.17.cloned.1.call-done.rows_ref), kind=kOutput, calls=%fused_computation.215 | convolution fusion | flops 9680453632 | bytes 28594176 | tf_op jit(solution)/shard_map/tc,cp->tp/dot_general | solution.py:26
  623.8 12.6 %fusion.136 = f32[577,4096]{1,0:T(8,128)} fusion(bf16[577,2048]{1,0:T(8,128)(2,1)S(1)} %get-tuple-element.125, bf16[2048,4096]{1,0:T(8,128)(2,1)S(1)} %bitcast.293), kind=kOutput, calls=%fused_computation.214 | convolution fusion | flops 9680453632 | bytes 28594176 | tf_op jit(solution)/shard_map/tc,cp->tp/dot_general | solution.py:26
  636.7 1.8 copy.37
  638.5 1.6 convert_element_type.141
  640.1 2.7 fusion.132
  642.8 20.0 %fusion.27 = bf16[1,577,4096]{2,1,0:T(8,128)(2,1)} fusion(bf16[577,2048]{1,0:T(8,128)(2,1)S(1)} %copy-done.30, bf16[2048,4096]{1,0:T(8,128)(2,1)} %all-gather.19.cloned.1.call-done.rows_ref, f32[577,4096]{1,0:T(8,128)} %fusion.137, f32[577,4096]{1,0:T(8,128)} %fusion.136, f32[4096]{0:T(1024)S(1)} %copy-done.47), kind=kOutput, calls=%fused_computation.49 | convolution fusion | flops 9689907200 | bytes 42790912 | tf_op jit(solution)/shard_map/tc,cp->tp/dot_general | solution.py:26
  662.8 80.8 %shard_map.267 = bf16[8,5,584,1024]{3,2,1,0:T(8,128)(2,1)} custom-call(bf16[8,577,4096]{2,1,0:T(8,128)(2,1)} %copy.35.grad_ref, bf16[2048,4096]{1,0:T(8,128)(2,1)} %all-gather.19.cloned.1.call-done.rows_ref, bf16[8,5,584,1024]{3,2,1,0:T(8,128)(2,1)} %shard_map.264.rest_0_), custom_call_target="tpu_custom_call", output_to_operand_aliasing={{}: (2, {})} | custom-call | flops 68585259008 | bytes 71335936 | tf_op jit(solution)/shard_map/pallas_call | solution.py:152
  744.9 8.6 %slice.288 = bf16[8,584,1024]{2,1,0:T(8,128)(2,1)} slice(bf16[8,632,1024]{2,1,0:T(8,128)(2,1)} %bitcast.286), slice={[0:8], [0:584], [0:1024]} | slice | bytes 19136512 | tf_op jit(solution)/shard_map/slice | solution.py:313
  (186 shorter events, 18.7 us)
Async XLA Ops:
  7.2 76.0 %all-gather.13.cloned.1.call-start = ((), (), s32[]{:S(2)}) async-start(), calls=%async_computation.4 | async-start | bytes 9437184 | tf_op jit(solution)/shard_map/all_gather | solution.py:210
  9.8 132.2 %all-gather.15.cloned.1.call-start = ((), (), s32[]{:S(2)}) async-start(), calls=%async_computation.5 | async-start | bytes 18874368 | tf_op jit(solution)/shard_map/all_gather | solution.py:211
  12.0 213.6 %all-gather.11.cloned.1.call-start = ((), (), s32[]{:S(2)}) async-start(), calls=%async_computation.3 | async-start | bytes 18874368 | tf_op jit(solution)/shard_map/all_gather | solution.py:215
  36.9 105.1 %copy-start.37 = (f32[8,1,512]{2,1,0:T(1,128)}, f32[8,1,512]{2,1,0:T(1,128)S(1)}, u32[]{:S(2)}) copy-start(f32[8,1,512]{2,1,0:T(1,128)S(1)} %all-gather.2) | copy-start | bytes 49156
  70.8 3.4 copy-start.39
  74.2 8.9 %copy-start.25 = (f32[584]{0:T(1024)}, f32[584]{0:T(1024)S(1)}, u32[]{:S(2)}) copy-start(f32[584]{0:T(1024)S(1)} %fusion.119) | copy-start | bytes 7012
  74.3 67.7 %copy-start.23 = (f32[1,1024]{1,0:T(1,128)}, f32[1,1024]{1,0:T(1,128)S(1)}, u32[]{:S(2)}) copy-start(f32[1,1024]{1,0:T(1,128)S(1)} %get-tuple-element.160) | copy-start | bytes 12292
  74.3 67.7 %copy-start.42 = (f32[1,1024]{1,0:T(1,128)}, f32[1,1024]{1,0:T(1,128)S(1)}, u32[]{:S(2)}) copy-start(f32[1,1024]{1,0:T(1,128)S(1)} %get-tuple-element.163) | copy-start | bytes 12292
  76.6 9.2 %copy-start.12 = (bf16[584,1024]{1,0:T(8,128)(2,1)}, bf16[584,1024]{1,0:T(8,128)(2,1)S(1)}, u32[]{:S(2)}) copy-start(bf16[584,1024]{1,0:T(8,128)(2,1)S(1)} %fusion.49) | copy-start | bytes 3588100
  83.1 225.3 %all-gather.17.cloned.1.call-start = ((), (), s32[]{:S(2)}) async-start(), calls=%async_computation.6 | async-start | bytes 18874368 | tf_op jit(solution)/shard_map/all_gather | solution.py:215
  83.8 313.0 %all-gather.19.cloned.1.call-start = ((), (), s32[]{:S(2)}) async-start(), calls=%async_computation.7 | async-start | bytes 18874368 | tf_op jit(solution)/shard_map/all_gather | solution.py:215
  94.8 19.7 %copy-start.2 = (bf16[584,4096]{1,0:T(8,128)(2,1)}, bf16[584,4096]{1,0:T(8,128)(2,1)S(1)}, u32[]{:S(2)}) copy-start(bf16[584,4096]{1,0:T(8,128)(2,1)S(1)} %convolution_convert_fusion.2.q_ref.k_ref.v_ref) | copy-start | bytes 14352388
  114.5 5.3 copy-start
  119.8 52.6 %copy-start.4 = (bf16[584,1024]{1,0:T(8,128)(2,1)}, bf16[584,1024]{1,0:T(8,128)(2,1)S(1)}, u32[]{:S(2)}) copy-start(bf16[584,1024]{1,0:T(8,128)(2,1)S(1)} %get-tuple-element.116) | copy-start | bytes 3588100
  119.8 52.6 %copy-start.19 = (f32[584]{0:T(1024)}, f32[584]{0:T(1024)S(1)}, u32[]{:S(2)}) copy-start(f32[584]{0:T(1024)S(1)} %broadcast_multiply_fusion) | copy-start | bytes 7012
  120.9 51.5 %copy-start.31 = (f32[584]{0:T(1024)}, f32[584]{0:T(1024)S(1)}, u32[]{:S(2)}) copy-start(f32[584]{0:T(1024)S(1)} %fusion.120) | copy-start | bytes 7012
  141.9 32.6 %copy-start.40 = (f32[1024]{0:T(1024)S(1)}, f32[1024]{0:T(1024)}, u32[]{:S(2)}) copy-start(f32[1024]{0:T(1024)} %param.27) | copy-start | bytes 12292
  141.9 32.6 %copy-start.46 = (bf16[2,4096,1024]{2,1,0:T(8,128)(2,1)S(1)}, bf16[2,4096,1024]{2,1,0:T(8,128)(2,1)}, u32[]{:S(2)}) copy-start(bf16[2,4096,1024]{2,1,0:T(8,128)(2,1)} %all-gather.15.cloned.1.call-done) | copy-start | bytes 50331652
  225.6 314.8 %all-gather.21.cloned.1.call-start = ((), (), s32[]{:S(2)}) async-start(), calls=%async_computation.11 | async-start | bytes 10764288 | tf_op jit(solution)/shard_map/all_gather | solution.py:257
  308.5 291.5 %reduce-scatter.4.cloned.1.call-start = ((), (), s32[]{:S(2)}) async-start(), calls=%async_computation.8 | async-start | bytes 9437184 | tf_op jit(solution)/shard_map/reduce_scatter | solution.py:276
  396.7 14.5 %slice-start.8 = ((s8[4784128]{0:T(1024)(128)(4,1)}), s8[4194304]{0:T(1024)(128)(4,1)S(1)}, s32[]{:S(2)}) async-start(s8[4784128]{0:T(1024)(128)(4,1)} %bitcast.328), calls=%async_computation.21 | async-start | bytes 8388608
  399.2 12.0 %slice-start.9 = ((s8[4784128]{0:T(1024)(128)(4,1)}), s8[589824]{0:T(1024)(128)(4,1)S(1)}, s32[]{:S(2)}) async-start(s8[4784128]{0:T(1024)(128)(4,1)} %bitcast.328), calls=%async_computation.22 | async-start | bytes 1179648
  411.2 9.3 %copy-start.14 = (bf16[577,1024]{1,0:T(8,128)(2,1)}, bf16[577,1024]{1,0:T(8,128)(2,1)S(1)}, u32[]{:S(2)}) copy-start(bf16[577,1024]{1,0:T(8,128)(2,1)S(1)} %fusion.77) | copy-start | bytes 3545092
  411.2 9.3 %copy-start.38 = (f32[8,1,512]{2,1,0:T(1,128)S(1)}, f32[8,1,512]{2,1,0:T(1,128)}, u32[]{:S(2)}) copy-start(f32[8,1,512]{2,1,0:T(1,128)} %copy-done.37) | copy-start | bytes 49156
  437.4 9.2 %copy-start.5 = (bf16[584,1024]{1,0:T(8,128)(2,1)S(1)}, bf16[584,1024]{1,0:T(8,128)(2,1)}, u32[]{:S(2)}) copy-start(bf16[584,1024]{1,0:T(8,128)(2,1)} %copy-done.4) | copy-start | bytes 3588100
  437.4 9.2 %copy-start.20 = (f32[584]{0:T(1024)S(1)}, f32[584]{0:T(1024)}, u32[]{:S(2)}) copy-start(f32[584]{0:T(1024)} %copy-done.19) | copy-start | bytes 7012
  437.4 9.3 %copy-start.24 = (f32[1,1024]{1,0:T(1,128)S(1)}, f32[1,1024]{1,0:T(1,128)}, u32[]{:S(2)}) copy-start(f32[1,1024]{1,0:T(1,128)} %copy-done.23) | copy-start | bytes 12292
  437.4 9.3 %copy-start.32 = (f32[584]{0:T(1024)S(1)}, f32[584]{0:T(1024)}, u32[]{:S(2)}) copy-start(f32[584]{0:T(1024)} %copy-done.31) | copy-start | bytes 7012
  437.4 9.3 %copy-start.43 = (f32[1,1024]{1,0:T(1,128)S(1)}, f32[1,1024]{1,0:T(1,128)}, u32[]{:S(2)}) copy-start(f32[1,1024]{1,0:T(1,128)} %copy-done.42) | copy-start | bytes 12292
  437.4 9.3 %copy-start.49 = (bf16[584,4096]{1,0:T(8,128)(2,1)S(1)}, bf16[584,4096]{1,0:T(8,128)(2,1)}, u32[]{:S(2)}) copy-start(bf16[584,4096]{1,0:T(8,128)(2,1)} %get-tuple-element.172) | copy-start | bytes 14352388
  456.4 143.5 %reduce-scatter.6.cloned.1.call-start = ((), (), s32[]{:S(2)}) async-start(), calls=%async_computation.9 | async-start | bytes 9437184 | tf_op jit(solution)/shard_map/reduce_scatter | solution.py:275
  457.3 182.8 %reduce-scatter.8.cloned.1.call-start = ((), (), s32[]{:S(2)}) async-start(), calls=%async_computation.10 | async-start | bytes 9437184 | tf_op jit(solution)/shard_map/reduce_scatter | solution.py:287
  459.7 4.6 copy-start.1
  464.3 3.2 copy-start.8
  464.3 6.3 slice-start
  470.6 38.4 %copy-start.13 = (bf16[584,1024]{1,0:T(8,128)(2,1)S(1)}, bf16[584,1024]{1,0:T(8,128)(2,1)}, u32[]{:S(2)}) copy-start(bf16[584,1024]{1,0:T(8,128)(2,1)} %copy-done.12) | copy-start | bytes 3588100
  520.2 223.4 %all-gather.23.cloned.1.call-start = ((), (), s32[]{:S(2)}) async-start(), calls=%async_computation.12 | async-start | bytes 11649024 | tf_op jit(solution)/shard_map/all_gather | solution.py:312
  520.5 5.0 copy-start.22
  520.6 5.0 copy-start.28
  525.5 8.5 %copy-start.34 = (f32[584]{0:T(1024)S(1)}, f32[584]{0:T(1024)}, u32[]{:S(2)}) copy-start(f32[584]{0:T(1024)} %copy-done.33) | copy-start | bytes 7012
  525.6 8.5 %copy-start.26 = (f32[584]{0:T(1024)S(1)}, f32[584]{0:T(1024)}, u32[]{:S(2)}) copy-start(f32[584]{0:T(1024)} %copy-done.25) | copy-start | bytes 7012
  550.8 49.1 %copy-start.7 = (bf16[584,1024]{1,0:T(8,128)(2,1)S(1)}, bf16[584,1024]{1,0:T(8,128)(2,1)}, u32[]{:S(2)}) copy-start(bf16[584,1024]{1,0:T(8,128)(2,1)} %fusion.60) | copy-start | bytes 3588100
  601.2 3.6 copy-start.6
  605.5 18.3 %slice-start.4 = ((s8[16777216]{0:T(1024)(128)(4,1)}), s8[4194304]{0:T(1024)(128)(4,1)S(1)}, s32[]{:S(2)}) async-start(s8[16777216]{0:T(1024)(128)(4,1)} %bitcast.292), calls=%async_computation.17 | async-start | bytes 8388608
  607.3 16.5 %slice-start.5 = ((s8[16777216]{0:T(1024)(128)(4,1)}), s8[4194304]{0:T(1024)(128)(4,1)S(1)}, s32[]{:S(2)}) async-start(s8[16777216]{0:T(1024)(128)(4,1)} %bitcast.292), calls=%async_computation.18 | async-start | bytes 8388608
  607.3 16.5 %slice-start.6 = ((s8[16777216]{0:T(1024)(128)(4,1)}), s8[4194304]{0:T(1024)(128)(4,1)S(1)}, s32[]{:S(2)}) async-start(s8[16777216]{0:T(1024)(128)(4,1)} %bitcast.292), calls=%async_computation.19 | async-start | bytes 8388608
  607.3 16.5 %slice-start.7 = ((s8[16777216]{0:T(1024)(128)(4,1)}), s8[4194304]{0:T(1024)(128)(4,1)S(1)}, s32[]{:S(2)}) async-start(s8[16777216]{0:T(1024)(128)(4,1)} %bitcast.292), calls=%async_computation.20 | async-start | bytes 8388608
  623.8 12.6 %copy-start.15 = (bf16[512,1024]{1,0:T(8,128)(2,1)S(1)}, bf16[512,1024]{1,0:T(8,128)(2,1)}, u32[]{:S(2)}) copy-start(bf16[512,1024]{1,0:T(8,128)(2,1)} %reduce-scatter.4.cloned.1.call-done) | copy-start | bytes 3145732
  (22 other events, 43.3 us)
Sparse Core Ops, SparseCore 0:
  10.2 48.5 all-gather.12
  60.9 80.9 all-gather.14
  144.1 81.3 all-gather.10
  227.0 81.3 all-gather.16
  310.5 81.3 all-gather.18
  393.3 51.0 all-gather.20
  456.6 47.4 reduce-scatter.3
  506.3 47.9 reduce-scatter.5
  556.6 47.9 reduce-scatter.7
  606.1 53.4 all-gather.22

commit v3 on v2

--- a/solution.py
+++ b/solution.py
@@ -35,7 +35,7 @@
     key_ok = lax.broadcasted_iota(jnp.int32, scores.shape, 1) < real_rows
     scores = jnp.where(key_ok, scores * q_act.shape[1] ** -0.5, -1e30)
     raised = jnp.exp(scores - jnp.max(scores, axis=-1, keepdims=True))
-    return raised / jnp.sum(raised, axis=-1, keepdims=True)
+    return raised * (1.0 / jnp.sum(raised, axis=-1, keepdims=True))
 
 
 def pad_keys(pads, refs):
@@ -65,11 +65,11 @@
         grad_p = lax.dot_general(grad, v_pad[:, cols], (((1,), (1,)), ((), ())), preferred_element_type=jnp.float32)
         grad_p = grad_p.astype(jnp.bfloat16).astype(jnp.float32)
         centre = jnp.sum(probs * grad_p, axis=-1, keepdims=True)
-        grad_s = (probs * (grad_p - centre) * head_dim ** -0.5).astype(jnp.bfloat16)
+        grad_s = (probs * (grad_p - centre)).astype(jnp.bfloat16)
         grad_k = lax.dot_general(grad_s, q_act, over_rows, preferred_element_type=jnp.float32)
         grad_q = jnp.dot(grad_s, k_pad[:, cols], preferred_element_type=jnp.float32)
-        out_ref[0, :, cols] = grad_q.astype(jnp.bfloat16)
-        out_ref[1, :, cols] = grad_k[0:tokens].astype(jnp.bfloat16)
+        out_ref[0, :, cols] = (grad_q * head_dim ** -0.5).astype(jnp.bfloat16)
+        out_ref[1, :, cols] = (grad_k[0:tokens] * head_dim ** -0.5).astype(jnp.bfloat16)
         out_ref[2, :, cols] = grad_v[0:tokens].astype(jnp.bfloat16)
 
 
@@ -165,29 +165,30 @@
 
 def rows_grad_kernel(real_rows, step, feats_ref, grad_ref, out_ref):
     tile = pl.program_id(0)
-    tokens, depth = grad_ref.shape[1:]
+    pair, tokens, depth = grad_ref.shape
 
     @pl.when(tile == 0)
     def _():
         out_ref[...] = jnp.zeros_like(out_ref)
 
-    is_real = lax.broadcasted_iota(jnp.int32, (tokens, step), 0) < real_rows
-    turned = feats_ref[0].T
+    is_real = lax.broadcasted_iota(jnp.int32, (pair, tokens, step), 1) < real_rows
+    turned = feats_ref[...].reshape(pair * tokens, -1).T
     for at in range(0, depth, step):
         cols = pl.ds(at, step)
-        grad = jnp.where(is_real, grad_ref[0, :, cols], jnp.bfloat16(0))
+        grad = jnp.where(is_real, grad_ref[:, :, cols], jnp.bfloat16(0)).reshape(pair * tokens, step)
         out_ref[:, cols] += jnp.dot(turned, grad, preferred_element_type=jnp.float32)
 
 
 def rows_grad(feats_local, grad):
     tiles, tokens, local = feats_local.shape
     real_rows, depth = grad.shape[1:]
+    pair = 2 - tiles % 2
     return pl.pallas_call(
         functools.partial(rows_grad_kernel, real_rows, min(512, depth)),
-        grid=(tiles,),
+        grid=(tiles // pair,),
         out_shape=jax.ShapeDtypeStruct((local, depth), jnp.float32),
-        in_specs=[pl.BlockSpec((1, tokens, local), lambda b: (b, 0, 0)),
-                  pl.BlockSpec((1, tokens, depth), lambda b: (b, 0, 0))],
+        in_specs=[pl.BlockSpec((pair, tokens, local), lambda b: (b, 0, 0)),
+                  pl.BlockSpec((pair, tokens, depth), lambda b: (b, 0, 0))],
         out_specs=pl.BlockSpec((local, depth), lambda b: (0, 0)),
         compiler_params=pltpu.CompilerParams(dimension_semantics=("arbitrary",), vmem_limit_bytes=58 * 1024 * 1024),
         cost_estimate=pl.CostEstimate(flops=2 * tiles * tokens * local * depth, bytes_accessed=2 * (feats_local.size + grad.size) + 4 * local * depth, transcendentals=0),
@@ -208,8 +209,7 @@
 
     flip = lambda w: w.reshape(width, local_width).T
     w_attn = lax.all_gather(jnp.stack([flip(w_query), flip(w_key), flip(w_value), w_out.reshape(local_width, width)]), 'tp', axis=1, tiled=True)
-    w_mlp = lax.all_gather(jnp.stack([w_fc1.T, w_fc2]), 'tp', axis=1, tiled=True)
-    fc1, fc2 = w_mlp[0], w_mlp[1]
+    mlp_part = jnp.stack([w_fc1.T, w_fc2])
     bias1 = lax.all_gather(b_fc1, 'tp', axis=0, tiled=True)
     proj_grad, bias1 = after(proj_grad, bias1)
     gather_rows = lambda part: lax.all_gather(part, 'tp', axis=0, tiled=True)
@@ -218,20 +218,18 @@
     x_wide = lax.dynamic_index_in_dim(hidden, mine, 0, keepdims=False).astype(jnp.float32)
     normed, norm1_pull = jax.vjp(layer_norm, x_wide, ln_params[0], ln_params[1])
     proj_grad = with_layout_constraint(proj_grad, Layout((0, 1, 2)))
-    normed, (proj_grad, w_parts[0]) = after(normed, (proj_grad, w_parts[0]))
+    normed, proj_grad = after(normed, proj_grad)
     proj_rows = [gather_rows(w_parts[0])]
+    w_mlp = lax.all_gather(mlp_part, 'tp', axis=1, tiled=True)
     qkv = matmul('td,jd->tj', normed, w_attn.reshape(-1, width)).astype(jnp.bfloat16)
     context = attend(real_rows, head_dim, width, qkv)
+    w_parts[1], context = after(w_parts[1], context)
+    proj_rows.append(gather_rows(w_parts[1]))
     attn_out = matmul('tj,jd->td', context, w_attn[3])
     gate_attn = jnp.tanh(gate_params[0])
     gate_mlp = jnp.tanh(gate_params[1])
     x_one_wide = (x_wide + gate_attn * attn_out).astype(jnp.bfloat16).astype(jnp.float32)
     normed_two, norm2_pull = jax.vjp(layer_norm, x_one_wide, ln_params[2], ln_params[3])
-    pre_act = matmul('td,fd->tf', normed_two, fc1) + bias1
-    mlp_act, gelu_pull = jax.vjp(gelu_bf16, pre_act)
-    mlp_out = matmul('tf,fd->td', mlp_act, fc2) + b_fc2
-    x_two = (x_one_wide + gate_mlp * mlp_out).astype(jnp.bfloat16)
-
     inter = jnp.transpose(inter_feats, (0, 2, 1, 3))
     grad_mine = lax.dynamic_index_in_dim(proj_grad, mine, 0, keepdims=False)
 
@@ -243,13 +241,28 @@
                 blocks.append((d, at // per_feat - 1, at % per_feat))
         return grad_feats_part(proj_grad, proj_rows[j], tuple(blocks), piece, feats, tokens, width, prior)
 
-    w_parts[1], w_attn = after(w_parts[1], w_attn)
-    proj_rows.append(gather_rows(w_parts[1]))
-    proj_rows[0], x_two = after(proj_rows[0], x_two)
+    grad_inter = feats_part(0, None)
+    w_mlp, grad_inter = after(w_mlp, grad_inter)
+    fc1, fc2 = w_mlp[0], w_mlp[1]
+    pre_act = matmul('td,fd->tf', normed_two, fc1) + bias1
+    mlp_act, gelu_pull = jax.vjp(gelu_bf16, pre_act)
+    mlp_out = matmul('tf,fd->td', mlp_act, fc2) + b_fc2
+    x_two = (x_one_wide + gate_mlp * mlp_out).astype(jnp.bfloat16)
+
     for part in w_parts[2:]:
-        part, proj_rows[0] = after(part, proj_rows[0])
+        part, x_two = after(part, x_two)
         proj_rows.append(gather_rows(part))
-    grad_inter = feats_part(0, None)
+    inter_mine = lax.dynamic_index_in_dim(inter, mine, 0, keepdims=False)
+    feats_mine = jnp.concatenate([x_two[None], inter_mine], axis=0)[:, :real_rows]
+
+    def proj_term(j):
+        part = jnp.concatenate([feats_mine[at // per_feat, :, (at % per_feat) * piece:(at % per_feat + 1) * piece]
+                                for at in range(j, group * per_dev, per_dev)], axis=-1)
+        return matmul('tc,cp->tp', part, proj_rows[j])
+
+    proj_sum = b_proj + proj_term(0)
+    grad_b_proj = jnp.sum(grad_mine, axis=0, dtype=jnp.float32)
+    proj_rows[1], (proj_sum, grad_b_proj) = after(proj_rows[1], (proj_sum, grad_b_proj))
     for j in range(1, per_dev - 1):
         proj_rows[j], grad_inter = after(proj_rows[j], grad_inter)
         grad_inter = feats_part(j, grad_inter)
@@ -300,7 +313,6 @@
         cols.append(jnp.where(feat == 0, from_two, from_inter))
     grad_w_proj = rows_grad(jnp.concatenate(cols, axis=-1), proj_grad)
 
-    grad_b_proj = jnp.sum(grad_mine, axis=0, dtype=jnp.float32)
     small = [grad_gain, grad_bias, grad_gain_two, grad_bias_two, grad_b_fc2, grad_b_fc1, grad_b_proj, jnp.stack([grad_gate_attn, grad_gate_mlp])]
     lines = [-(-v.shape[0] // width) for v in small]
     ends = [sum(lines[:n + 1]) for n in range(len(small))]
@@ -320,13 +332,8 @@
 
     proj_rows[-1], grad_tile = after(proj_rows[-1], grad_tile)
     grad_inter = jnp.transpose(feats_part(per_dev - 1, grad_inter), (0, 2, 1, 3))
-    inter_mine = lax.dynamic_index_in_dim(inter, mine, 0, keepdims=False)
-    feats_mine = jnp.concatenate([x_two[None], inter_mine], axis=0)[:, :real_rows]
-    proj_sum = b_proj
-    for j in range(per_dev):
-        part = jnp.concatenate([feats_mine[at // per_feat, :, (at % per_feat) * piece:(at % per_feat + 1) * piece]
-                                for at in range(j, group * per_dev, per_dev)], axis=-1)
-        proj_sum = proj_sum + matmul('tc,cp->tp', part, proj_rows[j])
+    for j in range(1, per_dev):
+        proj_sum = proj_sum + proj_term(j)
     proj_out = proj_sum.astype(jnp.bfloat16)[None]
     return (proj_out, grad_hidden, grad_inter, unflip(grad_w_attn[0]), unflip(grad_w_attn[1]), unflip(grad_w_attn[2]), grad_w_attn[3].reshape(local_heads, head_dim, width), grad_ln, grad_gates, grad_w_fc1, grad_b_fc1, grad_w_fc2, grad_b_fc2, grad_w_proj, grad_b_proj)
 

time: 773 us -> 748 us (0.968)
  waiting for transfers between devices: 78 us -> 52.4 us
    all_gather x3, waiting for transfers between devices: 55.2 us -> 38.7 us  [local_step(): gather_rows = lambda part: lax.all_gather(part, 'tp', axis=0, tiled=True)]
    all_gather x1, waiting for transfers between devices: 21 us -> 12.4 us  [local_step(): w_mlp = lax.all_gather(mlp_part, 'tp', axis=1, tiled=True)]
  transfers between devices with their start and end apart: 10 -> 10, of which waited for: 3 -> 3; matrix products, arithmetic and copies ran while one was open for 36% -> 38% of each run, Pallas kernels for 45% -> 45%
where the time goes in v3:
time: 748 us; the launch traced here: 739 us
  Pallas kernels  335 us (45%)
  matrix products  183 us (24%)
  local copies, waits for them, and re-layouts  78.4 us (10%)
  waiting for transfers between devices  52.4 us (7%)
  other arithmetic  45.4 us (6%)
  blocking collectives  25.1 us (3%)
  between operations  18 us (2%)
    pallas_call x3, Pallas kernels, grad_feats_part(): pl.pallas_call(functools.partial(feats_kernel, blocks, piece, real_rows),...  236 us
    dot_general x16, matrix products, matmul(): jnp.einsum(eq_form, lhs_in, rhs_in, preferred_element_type=jnp.float32)  183 us
    pallas_call x2, Pallas kernels, attend(): pl.pallas_call(functools.partial(kernel, real_rows, head_dim), grid=(step...  56.2 us
    pallas_call x1, Pallas kernels, rows_grad(): pl.pallas_call(functools.partial(rows_grad_kernel, real_rows, min(512, de...  43.3 us
    all_gather x3, waiting for transfers between devices, local_step(): gather_rows = lambda part: lax.all_gather(part, 'tp', axis=0, tiled=True)  38.7 us
    optimization_barrier x1, local copies, waits for them, and re-layouts, after(): return lax.optimization_barrier((value, earlier))  33.9 us
    all_gather x1, blocking collectives, local_step(): bias1 = lax.all_gather(b_fc1, 'tp', axis=0, tiled=True)  25.1 us
  transfers between devices with their start and end apart: 10, of which 3 were waited for; matrix products, arithmetic and copies ran while one was open for 38% of the time, Pallas kernels for 45%

profile of v3, /device:TPU:112, one launch (start us, length us, event | category | flops | bytes accessed | tf_op | source)
XLA Modules:
  0.0 738.7 jit_solution(8096156876136274849)
XLA Ops:
  7.3 2.3 pad_maximum_fusion.4
  9.7 5.8 fusion.141
  17.2 1.5 pad_maximum_fusion.2
  18.9 25.1 %all-gather.2 = f32[8,1,512]{2,1,0:T(1,128)S(1)} all-gather(f32[1,1,512]{2,1,0:T(1,128)S(1)} %bitcast.323), channel_id=1, replica_groups=mesh['dp'=2,'tp'=8] {'tp'}, dimensions={0}, use_global_device_ids=true | all-gather | bytes 18432 | tf_op jit(solution)/shard_map/all_gather | solution.py:213
  44.0 33.9 %copy.35.grad_ref = bf16[8,577,4096]{2,1,0:T(8,128)(2,1)} copy(bf16[8,577,4096]{2,0,1:T(8,128)(2,1)} %param.17) | data formatting | bytes 75628544 | tf_op jit(solution)/shard_map/optimization_barrier | solution.py:30
  77.9 1.5 convert_reduce_fusion.4
  79.5 1.8 fusion.62
  81.9 1.8 fusion.61
  84.7 9.0 %convolution_convert_fusion.2.q_ref.k_ref.v_ref = bf16[584,4096]{1,0:T(8,128)(2,1)S(1)} fusion(bf16[584,1024]{1,0:T(8,128)(2,1)S(1)} %fusion.61, bf16[4096,1024]{1,0:T(8,128)(2,1)} %bitcast.324), kind=kOutput, calls=%fused_computation.54 | convolution fusion | flops 4901339136 | bytes 14368768 | tf_op jit(solution)/shard_map/td,jd->tj/dot_general | solution.py:26
  93.7 19.7 %shard_map.262 = bf16[584,1024]{1,0:T(8,128)(2,1)S(1)} custom-call(bf16[584,4096]{1,0:T(8,128)(2,1)S(1)} %convolution_convert_fusion.2.q_ref.k_ref.v_ref, bf16[584,4096]{1,0:T(8,128)(2,1)S(1)} %convolution_convert_fusion.2.q_ref.k_ref.v_ref, bf16[584,4096]{1,0:T(8,128)(2,1)S(1)} %convolution_convert_fusion.2.q_ref.k_ref.v_ref), custom_call_target="tpu_custom_call" | custom-call | flops 6123683840 | bytes 9568256 | tf_op jit(solution)/shard_map/pallas_call | solution.py:91
  115.7 4.8 convert_reduce_fusion.3
  121.0 20.9 %all-gather.17.cloned.1.call-done.rows_ref = bf16[2048,4096]{1,0:T(8,128)(2,1)} async-done(((bf16[256,4096]{1,0:T(8,128)(2,1)}), bf16[2048,4096]{1,0:T(8,128)(2,1)}) %all-gather.17.cloned.1.call-update) | async-done | bytes 16777232 | tf_op jit(solution)/shard_map/all_gather | solution.py:215
  142.0 71.2 %shard_map.263.rest_0_ = bf16[8,5,584,1024]{3,2,1,0:T(8,128)(2,1)} custom-call(bf16[8,577,4096]{2,1,0:T(8,128)(2,1)} %copy.35.grad_ref, bf16[2048,4096]{1,0:T(8,128)(2,1)} %all-gather.17.cloned.1.call-done.rows_ref), custom_call_target="tpu_custom_call" | custom-call | flops 58787364864 | bytes 68943872 | tf_op jit(solution)/shard_map/pallas_call | solution.py:152
  213.2 12.4 %all-gather.15.cloned.1.call-done = bf16[2,4096,1024]{2,1,0:T(8,128)(2,1)} async-done(((bf16[2,512,1024]{2,1,0:T(8,128)(2,1)}), bf16[2,4096,1024]{2,1,0:T(8,128)(2,1)}) %all-gather.15.cloned.1.call-update) | async-done | bytes 16777232 | tf_op jit(solution)/shard_map/all_gather | solution.py:223
  225.6 30.4 %multiply_convert_fusion = (bf16[584,4096]{1,0:T(8,128)(2,1)S(1)}, f32[584,4096]{1,0:T(8,128)}, f32[584,4096]{1,0:T(8,128)}) fusion(f32[4096]{0:T(1024)S(1)} %bitcast.317, bf16[2,4096,1024]{2,1,0:T(8,128)(2,1)} %all-gather.15.cloned.1.call-done, bf16[584,1024]{1,0:T(8,128)(2,1)S(1)} %get-tuple-element.120, f32[1024]{0:T(1024)S(1)} %bitcast.321, ...), kind=kOutput, calls=%fused_computation.12 | convolution fusion | flops 5060411392 | bytes 33534528 | tf_op jit(solution)/shard_map/td,fd->tf/dot_general | solution.py:26
  256.0 6.8 fusion.67
  262.9 4.4 convert_reduce_fusion
  267.4 3.6 dynamic-slice_bitcast_fusion
  274.8 15.9 %convolution_add_fusion = f32[577,4096]{1,0:T(8,128)} fusion(bf16[577,2048]{1,0:T(8,128)(2,1)S(1)} %get-tuple-element.131, bf16[2048,4096]{1,0:T(8,128)(2,1)} %all-gather.17.cloned.1.call-done.rows_ref, f32[4096]{0:T(1024)S(1)} %copy-done.47), kind=kOutput, calls=%fused_computation.50 | convolution fusion | flops 9682817024 | bytes 28610560 | tf_op jit(solution)/shard_map/tc,cp->tp/dot_general | solution.py:26
  290.6 17.8 %all-gather.13.cloned.1.call-done.rows_ref = bf16[2048,4096]{1,0:T(8,128)(2,1)} async-done(((bf16[256,4096]{1,0:T(8,128)(2,1)}), bf16[2048,4096]{1,0:T(8,128)(2,1)}) %all-gather.13.cloned.1.call-update) | async-done | bytes 16777232 | tf_op jit(solution)/shard_map/all_gather | solution.py:215
  308.6 4.7 fusion.140
  313.3 83.6 %shard_map.264.rest_0_ = bf16[8,5,584,1024]{3,2,1,0:T(8,128)(2,1)} custom-call(bf16[8,577,4096]{2,1,0:T(8,128)(2,1)} %copy.35.grad_ref, bf16[2048,4096]{1,0:T(8,128)(2,1)} %all-gather.13.cloned.1.call-done.rows_ref, bf16[8,5,584,1024]{3,2,1,0:T(8,128)(2,1)} %shard_map.263.rest_0_), custom_call_target="tpu_custom_call", output_to_operand_aliasing={{}: (2, {})} | custom-call | flops 68585259008 | bytes 71335936 | tf_op jit(solution)/shard_map/pallas_call | solution.py:152
  396.9 1.7 slice-done.2
  399.5 11.3 %fusion.87 = bf16[577,1024]{1,0:T(8,128)(2,1)S(1)} fusion(bf16[256,4096]{1,0:T(8,128)(2,1)} %get-tuple-element.125, bf16[256,4096]{1,0:T(8,128)(2,1)S(1)} %slice-done.3, bf16[256,4096]{1,0:T(8,128)(2,1)S(1)} %slice-done.2, bf16[256,4096]{1,0:T(8,128)(2,1)} %get-tuple-element.124, bf16[8,577,4096]{2,1,0:T(8,128)(2,1)} %copy.35.grad_ref, s32[]{:T(128)S(6)} %select_n.71), kind=kOutput, calls=%fused_computation.127 | convolution fusion | flops 4874372096 | bytes 14354436 | tf_op jit(solution)/shard_map/tp,cp->tc/dot_general | solution.py:26
  410.8 12.1 %convolution_convert_fusion = bf16[4096,1024]{1,0:T(8,128)(2,1)} fusion(bf16[584,4096]{1,0:T(8,128)(2,1)} %copy-done.48, f32[]{:T(128)} %bitcast.18, bf16[577,1024]{1,0:T(8,128)(2,1)S(1)} %fusion.87), kind=kOutput, calls=%fused_computation.43 | convolution fusion | flops 4904935424 | bytes 14354436 | tf_op jit(solution)/shard_map/tf,td->fd/dot_general | solution.py:26
  422.9 16.8 %fusion.145 = (f32[4096]{0:T(1024)S(1)}, bf16[584,4096]{1,0:T(8,128)(2,1)}) fusion(f32[584,4096]{1,0:T(8,128)} %get-tuple-element.118, bf16[2,4096,1024]{2,1,0:T(8,128)(2,1)} %all-gather.15.cloned.1.call-done, f32[]{:T(128)} %bitcast.18, bf16[577,1024]{1,0:T(8,128)(2,1)S(1)} %fusion.87, f32[584,4096]{1,0:T(8,128)} %get-tuple-element.171, ...), kind=kOutput, calls=%fused_computation.218 | convolution fusion | flops 4943794176 | bytes 33524224 | tf_op jit(solution)/shard_map/td,fd->tf/dot_general | solution.py:26
  439.8 9.2 %fusion.82 = bf16[584,1024]{1,0:T(8,128)(2,1)S(1)} fusion(bf16[2,4096,1024]{2,1,0:T(8,128)(2,1)} %all-gather.15.cloned.1.call-done, bf16[584,4096]{1,0:T(8,128)(2,1)} %get-tuple-element.176), kind=kOutput, calls=%fused_computation.126 | convolution fusion | flops 4899545088 | bytes 14368768 | tf_op jit(solution)/shard_map/tf,fd->td/dot_general | solution.py:26
  449.0 9.7 %convolution_convert_fusion.1 = bf16[4096,1024]{1,0:T(8,128)(2,1)} fusion(bf16[584,4096]{1,0:T(8,128)(2,1)S(1)} %copy-done.49, bf16[584,1024]{1,0:T(8,128)(2,1)S(1)} %copy-done.5, f32[1024]{0:T(1024)S(1)} %bitcast.322, f32[1024]{0:T(1024)S(1)} %bitcast.303, f32[584]{0:T(1024)S(1)} %copy-done.34, f32[584]{0:T(1024)S(1)} %copy-done.20), kind=kOutput, calls=%fused_computation.44 | convolution fusion | flops 4906729472 | bytes 14381632 | tf_op jit(solution)/shard_map/tf,td->fd/dot_general | solution.py:26
  462.0 4.2 fusion.69
  466.2 3.2 convert_bitcast_fusion.2
  469.4 3.1 fusion.81.grad_ref
  472.5 36.5 %shard_map.265 = bf16[3,584,1024]{2,1,0:T(8,128)(2,1)S(1)} custom-call(bf16[584,4096]{1,0:T(8,128)(2,1)S(1)} %bitcast.284, bf16[584,4096]{1,0:T(8,128)(2,1)S(1)} %bitcast.284, bf16[584,4096]{1,0:T(8,128)(2,1)S(1)} %bitcast.284, bf16[584,1024]{1,0:T(8,128)(2,1)S(1)} %fusion.81.grad_ref), custom_call_target="tpu_custom_call" | custom-call | flops 15309209600 | bytes 9568256 | tf_op jit(solution)/shard_map/pallas_call | solution.py:91
  509.1 1.8 copy-done.3
  510.9 5.5 convolution_convert_fusion.3
  516.4 5.6 pad_maximum_fusion
  524.1 8.4 %convert_reduce_fusion.1 = (f32[1024]{0:T(1024)S(1)}, f32[584]{0:T(1024)S(1)}, bf16[584,1024]{1,0:T(8,128)(2,1)S(1)}) fusion(f32[1024]{0:T(1024)S(1)} %bitcast.308, f32[584]{0:T(1024)S(1)} %copy-done.22, bf16[8,584,1024]{2,1,0:T(8,128)(2,1)} %param.15, s32[]{:T(128)S(6)} %select_n.71, bf16[3,584,1024]{2,1,0:T(8,128)(2,1)} %copy-done.3, ...), kind=kOutput, calls=%fused_computation.60 | convolution fusion | flops 3678992896 | bytes 12284484 | tf_op jit(solution)/shard_map/gtj,gjd->td/dot_general | solution.py:26
  532.5 2.7 fusion.74
  535.5 3.3 fusion.72
  538.8 7.2 bitcast_select_fusion.2
  546.0 3.4 pad_maximum_fusion.1.feats_ref
  549.4 43.3 %shard_map.266 = f32[768,4096]{1,0:T(8,128)} custom-call(bf16[8,584,768]{2,1,0:T(8,128)(2,1)} %pad_maximum_fusion.1.feats_ref, bf16[8,577,4096]{2,1,0:T(8,128)(2,1)} %copy.35.grad_ref), custom_call_target="tpu_custom_call" | custom-call | flops 29393682432 | bytes 57573376 | tf_op jit(solution)/shard_map/pallas_call | solution.py:186
  593.9 17.1 %fusion.146 = f32[577,4096]{1,0:T(8,128)} fusion(bf16[577,2048]{1,0:T(8,128)(2,1)} %copy-done.30, bf16[2048,4096]{1,0:T(8,128)(2,1)} %all-gather.13.cloned.1.call-done.rows_ref), kind=kOutput, calls=%fused_computation.219 | convolution fusion | flops 9680453632 | bytes 28594176 | tf_op jit(solution)/shard_map/tc,cp->tp/dot_general | solution.py:26
  611.3 1.8 copy.37
  613.1 1.6 convert_element_type.141
  614.7 2.9 fusion.142
  617.6 19.9 %fusion.37 = bf16[1,577,4096]{2,1,0:T(8,128)(2,1)} fusion(bf16[577,2048]{1,0:T(8,128)(2,1)S(1)} %copy-done.32, bf16[2048,4096]{1,0:T(8,128)(2,1)} %all-gather.19.cloned.1.call-done.rows_ref, f32[577,4096]{1,0:T(8,128)} %convolution_add_fusion, f32[577,4096]{1,0:T(8,128)} %fusion.146), kind=kOutput, calls=%fused_computation.56 | convolution fusion | flops 9687543808 | bytes 42774528 | tf_op jit(solution)/shard_map/tc,cp->tp/dot_general | solution.py:26
  637.5 81.1 %shard_map.267 = bf16[8,5,584,1024]{3,2,1,0:T(8,128)(2,1)} custom-call(bf16[8,577,4096]{2,1,0:T(8,128)(2,1)} %copy.35.grad_ref, bf16[2048,4096]{1,0:T(8,128)(2,1)} %all-gather.19.cloned.1.call-done.rows_ref, bf16[8,5,584,1024]{3,2,1,0:T(8,128)(2,1)} %shard_map.264.rest_0_), custom_call_target="tpu_custom_call", output_to_operand_aliasing={{}: (2, {})} | custom-call | flops 68585259008 | bytes 71335936 | tf_op jit(solution)/shard_map/pallas_call | solution.py:152
  719.9 8.6 %slice.286 = bf16[8,584,1024]{2,1,0:T(8,128)(2,1)} slice(bf16[8,632,1024]{2,1,0:T(8,128)(2,1)} %bitcast.286), slice={[0:8], [0:584], [0:1024]} | slice | bytes 19136512 | tf_op jit(solution)/shard_map/slice | solution.py:325
  (172 shorter events, 19.9 us)
Async XLA Ops:
  7.2 76.5 %all-gather.11.cloned.1.call-start = ((), (), s32[]{:S(2)}) async-start(), calls=%async_computation.3 | async-start | bytes 9437184 | tf_op jit(solution)/shard_map/all_gather | solution.py:211
  9.6 132.3 %all-gather.17.cloned.1.call-start = ((), (), s32[]{:S(2)}) async-start(), calls=%async_computation.6 | async-start | bytes 18874368 | tf_op jit(solution)/shard_map/all_gather | solution.py:215
  15.5 210.0 %all-gather.15.cloned.1.call-start = ((), (), s32[]{:S(2)}) async-start(), calls=%async_computation.5 | async-start | bytes 18874368 | tf_op jit(solution)/shard_map/all_gather | solution.py:223
  18.8 289.6 %all-gather.13.cloned.1.call-start = ((), (), s32[]{:S(2)}) async-start(), calls=%async_computation.4 | async-start | bytes 18874368 | tf_op jit(solution)/shard_map/all_gather | solution.py:215
  77.9 3.3 copy-start.39
  79.5 2.4 copy-start.21
  81.3 12.4 %copy-start.26 = (f32[584]{0:T(1024)}, f32[584]{0:T(1024)S(1)}, u32[]{:S(2)}) copy-start(f32[584]{0:T(1024)S(1)} %fusion.129) | copy-start | bytes 7012
  81.3 12.4 %copy-start.28 = (f32[1,1024]{1,0:T(1,128)}, f32[1,1024]{1,0:T(1,128)S(1)}, u32[]{:S(2)}) copy-start(f32[1,1024]{1,0:T(1,128)S(1)} %get-tuple-element.166) | copy-start | bytes 12292
  81.3 144.2 %copy-start.23 = (f32[1,1024]{1,0:T(1,128)}, f32[1,1024]{1,0:T(1,128)S(1)}, u32[]{:S(2)}) copy-start(f32[1,1024]{1,0:T(1,128)S(1)} %get-tuple-element.164) | copy-start | bytes 12292
  81.3 144.2 %copy-start.42 = (f32[1,1024]{1,0:T(1,128)}, f32[1,1024]{1,0:T(1,128)S(1)}, u32[]{:S(2)}) copy-start(f32[1,1024]{1,0:T(1,128)S(1)} %get-tuple-element.167) | copy-start | bytes 12292
  93.7 19.7 %copy-start.2 = (bf16[584,4096]{1,0:T(8,128)(2,1)}, bf16[584,4096]{1,0:T(8,128)(2,1)S(1)}, u32[]{:S(2)}) copy-start(bf16[584,4096]{1,0:T(8,128)(2,1)S(1)} %convolution_convert_fusion.2.q_ref.k_ref.v_ref) | copy-start | bytes 14352388
  93.7 19.8 %copy-start.45 = (f32[2]{0:T(128)S(1)}, f32[2]{0:T(128)}, u32[]{:S(2)}) copy-start(f32[2]{0:T(128)} %param.23) | copy-start | bytes 28
  113.4 7.1 copy-start
  113.5 283.4 %all-gather.19.cloned.1.call-start = ((), (), s32[]{:S(2)}) async-start(), calls=%async_computation.7 | async-start | bytes 18874368 | tf_op jit(solution)/shard_map/all_gather | solution.py:215
  120.5 135.5 %copy-start.4 = (bf16[584,1024]{1,0:T(8,128)(2,1)}, bf16[584,1024]{1,0:T(8,128)(2,1)S(1)}, u32[]{:S(2)}) copy-start(bf16[584,1024]{1,0:T(8,128)(2,1)S(1)} %get-tuple-element.120) | copy-start | bytes 3588100
  120.5 105.0 %copy-start.19 = (f32[584]{0:T(1024)}, f32[584]{0:T(1024)S(1)}, u32[]{:S(2)}) copy-start(f32[584]{0:T(1024)S(1)} %broadcast_multiply_fusion) | copy-start | bytes 7012
  121.0 92.2 %copy-start.37 = (f32[584]{0:T(1024)}, f32[584]{0:T(1024)S(1)}, u32[]{:S(2)}) copy-start(f32[584]{0:T(1024)S(1)} %fusion.65) | copy-start | bytes 7012
  121.0 104.5 %copy-start.33 = (f32[584]{0:T(1024)}, f32[584]{0:T(1024)S(1)}, u32[]{:S(2)}) copy-start(f32[584]{0:T(1024)S(1)} %fusion.130) | copy-start | bytes 7012
  225.6 30.4 %copy-start.40 = (f32[1024]{0:T(1024)S(1)}, f32[1024]{0:T(1024)}, u32[]{:S(2)}) copy-start(f32[1024]{0:T(1024)} %param.27) | copy-start | bytes 12292
  225.6 30.4 %copy-start.46 = (bf16[2,4096,1024]{2,1,0:T(8,128)(2,1)S(1)}, bf16[2,4096,1024]{2,1,0:T(8,128)(2,1)}, u32[]{:S(2)}) copy-start(bf16[2,4096,1024]{2,1,0:T(8,128)(2,1)} %all-gather.15.cloned.1.call-done) | copy-start | bytes 50331652
  256.0 6.8 copy-start.48
  262.8 8.2 %copy-start.6 = (bf16[584,1024]{1,0:T(8,128)(2,1)}, bf16[584,1024]{1,0:T(8,128)(2,1)S(1)}, u32[]{:S(2)}) copy-start(bf16[584,1024]{1,0:T(8,128)(2,1)S(1)} %get-tuple-element.61) | copy-start | bytes 3588100
  262.9 275.9 %all-gather.21.cloned.1.call-start = ((), (), s32[]{:S(2)}) async-start(), calls=%async_computation.11 | async-start | bytes 10764288 | tf_op jit(solution)/shard_map/all_gather | solution.py:270
  271.5 3.2 copy-start.47
  308.5 284.2 %reduce-scatter.4.cloned.1.call-start = ((), (), s32[]{:S(2)}) async-start(), calls=%async_computation.8 | async-start | bytes 9437184 | tf_op jit(solution)/shard_map/reduce_scatter | solution.py:289
  396.9 2.6 slice-start.3
  410.8 12.1 %copy-start.14 = (bf16[577,1024]{1,0:T(8,128)(2,1)}, bf16[577,1024]{1,0:T(8,128)(2,1)S(1)}, u32[]{:S(2)}) copy-start(bf16[577,1024]{1,0:T(8,128)(2,1)S(1)} %fusion.87) | copy-start | bytes 3545092
  439.7 9.2 %copy-start.5 = (bf16[584,1024]{1,0:T(8,128)(2,1)S(1)}, bf16[584,1024]{1,0:T(8,128)(2,1)}, u32[]{:S(2)}) copy-start(bf16[584,1024]{1,0:T(8,128)(2,1)} %copy-done.4) | copy-start | bytes 3588100
  439.7 9.2 %copy-start.20 = (f32[584]{0:T(1024)S(1)}, f32[584]{0:T(1024)}, u32[]{:S(2)}) copy-start(f32[584]{0:T(1024)} %copy-done.19) | copy-start | bytes 7012
  439.7 9.3 %copy-start.24 = (f32[1,1024]{1,0:T(1,128)S(1)}, f32[1,1024]{1,0:T(1,128)}, u32[]{:S(2)}) copy-start(f32[1,1024]{1,0:T(1,128)} %copy-done.23) | copy-start | bytes 12292
  439.7 9.3 %copy-start.34 = (f32[584]{0:T(1024)S(1)}, f32[584]{0:T(1024)}, u32[]{:S(2)}) copy-start(f32[584]{0:T(1024)} %copy-done.33) | copy-start | bytes 7012
  439.7 9.3 %copy-start.43 = (f32[1,1024]{1,0:T(1,128)S(1)}, f32[1,1024]{1,0:T(1,128)}, u32[]{:S(2)}) copy-start(f32[1,1024]{1,0:T(1,128)} %copy-done.42) | copy-start | bytes 12292
  439.7 9.3 %copy-start.49 = (bf16[584,4096]{1,0:T(8,128)(2,1)S(1)}, bf16[584,4096]{1,0:T(8,128)(2,1)}, u32[]{:S(2)}) copy-start(bf16[584,4096]{1,0:T(8,128)(2,1)} %get-tuple-element.176) | copy-start | bytes 14352388
  458.7 134.0 %reduce-scatter.6.cloned.1.call-start = ((), (), s32[]{:S(2)}) async-start(), calls=%async_computation.9 | async-start | bytes 9437184 | tf_op jit(solution)/shard_map/reduce_scatter | solution.py:288
  459.6 155.1 %reduce-scatter.8.cloned.1.call-start = ((), (), s32[]{:S(2)}) async-start(), calls=%async_computation.10 | async-start | bytes 9437184 | tf_op jit(solution)/shard_map/reduce_scatter | solution.py:300
  459.7 2.4 copy-start.11
  462.0 4.2 copy-start.1
  466.2 3.2 copy-start.8
  466.2 6.3 slice-start
  469.4 3.1 slice-start.1
  472.5 38.3 %copy-start.13 = (bf16[584,1024]{1,0:T(8,128)(2,1)S(1)}, bf16[584,1024]{1,0:T(8,128)(2,1)}, u32[]{:S(2)}) copy-start(bf16[584,1024]{1,0:T(8,128)(2,1)} %copy-done.12) | copy-start | bytes 3588100
  522.0 196.7 %all-gather.23.cloned.1.call-start = ((), (), s32[]{:S(2)}) async-start(), calls=%async_computation.12 | async-start | bytes 11649024 | tf_op jit(solution)/shard_map/all_gather | solution.py:324
  524.1 8.4 %copy-start.36 = (f32[584]{0:T(1024)S(1)}, f32[584]{0:T(1024)}, u32[]{:S(2)}) copy-start(f32[584]{0:T(1024)} %copy-done.35) | copy-start | bytes 7012
  524.1 8.5 %copy-start.27 = (f32[584]{0:T(1024)S(1)}, f32[584]{0:T(1024)}, u32[]{:S(2)}) copy-start(f32[584]{0:T(1024)} %copy-done.26) | copy-start | bytes 7012
  532.5 3.0 copy-start.9
  549.4 43.3 %copy-start.7 = (bf16[584,1024]{1,0:T(8,128)(2,1)S(1)}, bf16[584,1024]{1,0:T(8,128)(2,1)}, u32[]{:S(2)}) copy-start(bf16[584,1024]{1,0:T(8,128)(2,1)} %fusion.72) | copy-start | bytes 3588100
  593.9 17.1 %copy-start.15 = (bf16[512,1024]{1,0:T(8,128)(2,1)S(1)}, bf16[512,1024]{1,0:T(8,128)(2,1)}, u32[]{:S(2)}) copy-start(bf16[512,1024]{1,0:T(8,128)(2,1)} %reduce-scatter.4.cloned.1.call-done) | copy-start | bytes 3145732
  614.7 2.9 copy-start.32
  (16 other events, 25.1 us)
Sparse Core Ops, SparseCore 0:
  10.2 48.5 all-gather.10
  61.0 80.9 all-gather.16
  144.1 81.3 all-gather.14
  227.0 81.3 all-gather.12
  309.9 81.3 all-gather.18
  392.7 51.0 all-gather.20
  458.9 48.6 reduce-scatter.3
  509.9 47.9 reduce-scatter.5
  560.1 47.9 reduce-scatter.7
  609.6 53.4 all-gather.22
